TPU v7x, 32 devices: a whole 2x2x4 slice. The times are simulated.
32 devices in a mesh: req: 4 (over z), kvh: 4 (over y, core), exp: 2 (over x).
Axes of the slice: x: 2, y: 2, z: 4, core: 2. Of those that a mesh axis runs over, the one named last changes fastest.
Arguments:
- queries: bfloat16 [512, 2048], P(('req', 'exp'), 'kvh'), may hold values from -170 to 170
- keys: bfloat16 [512, 4, 64, 128], P(('req', 'exp'), 'kvh'), may hold values from -6 to 6
- values: bfloat16 [512, 4, 64, 128], P(('req', 'exp'), 'kvh'), may hold values from -6 to 6
- lengths: int32 [512], P('req'), may hold values from 2 to 64
- out_weight: bfloat16 [2048, 2048], P(('kvh', 'exp')), may hold values from -0.125 to 0.125
- residual: bfloat16 [512, 2048], P('req'), may hold values from -54 to 54
- norm_gain: float32 [2048], replicated, may hold values from 0.5 to 2
- expert_ids: int32 [512, 8], P('req'), may hold values from 0 to 7, as said below
- gate_weights: float32 [512, 8], P('req'), may hold values from 0.2 to 1
- replica_map: int32 [16], replicated, may hold values from 0 to 7, as said below
- w_gate: bfloat16 [16, 2048, 384], P(('req', 'kvh'), None, 'exp')
- w_up: bfloat16 [16, 2048, 384], P(('req', 'kvh'), None, 'exp')
- w_down: bfloat16 [16, 384, 2048], P(('req', 'kvh'), 'exp')
Outputs:
- layer_out: bfloat16 [512, 2048], P('req', ('kvh', 'exp'))
Inputs may be any that keep to these rules, and one draw needn't show every extreme that they name: `replica_map`: every one of the 8 experts is served by one or more slots; slots that serve one expert hold equal weights in w_gate, w_up and w_down. `expert_ids`: A token names 8 different experts and every expert is named by some token; among the 128 tokens of one req index no expert is named by more than 128 tokens, and in every req index some expert is named by exactly 128.
All inputs are finite; a program needn't handle non-finite values.
Results may differ from a plain program's by a relative error of at most 0.008.
Values may be sent and summed in bfloat16 or wider, within the bound.
No kernel may reach another device: no remote copies, remote signals or barrier semaphores. Data moves between devices by JAX's collectives and lax.ppermute only.
A program may use at most 64 MiB of HBM per device.

v0:
```python
import jax
import jax.numpy as jnp
from jax import lax
from jax.experimental import pallas as pl
from jax.experimental.pallas import tpu as pltpu
from jax.sharding import PartitionSpec as P


def swapped(value, axis, apart):
    mask = 2**apart
    pairs = [(source, source ^ mask) for source in range(lax.axis_size(axis))]
    return lax.ppermute(value, axis, pairs)


def expert_runner(w_gate, w_up, w_down, complete, n_kvh, n_exp, block):

    def run(received):
        full = complete(received)
        lead_a = full.shape[0]
        lead_b = full.shape[1]
        d_model = w_gate.shape[1]
        rows = full.reshape(lead_a * lead_b, d_model)
        gate = jnp.dot(rows, w_gate[0], preferred_element_type=jnp.float32)
        up = jnp.dot(rows, w_up[0], preferred_element_type=jnp.float32)
        act = (jax.nn.silu(gate) * up).astype(jnp.bfloat16)
        down = jnp.dot(act, w_down[0], preferred_element_type=jnp.float32)
        terms = down.reshape(lead_a, lead_b, n_kvh, n_exp, block)
        summed = lax.psum_scatter(
            terms.astype(jnp.bfloat16), "exp", scatter_dimension=3, tiled=True
        )
        back = summed.reshape(lead_a, lead_b, n_kvh * block)
        return lax.all_to_all(back, "req", split_axis=0, concat_axis=0, tiled=True)

    return run


def routed_shards(
    queries,
    keys,
    values,
    lengths,
    out_weight,
    residual,
    norm_gain,
    expert_ids,
    gate_weights,
    replica_map,
    w_gate,
    w_up,
    w_down,
):
    f32 = jnp.float32
    half_rows_count = queries.shape[0]
    n_rows = lengths.shape[0]
    head_dim = keys.shape[3]
    span = keys.shape[2]
    heads_here = queries.shape[1] // head_dim
    n_kvh = lax.axis_size("kvh")
    n_exp = lax.axis_size("exp")
    n_req = lax.axis_size("req")
    side = lax.axis_index("exp")
    own_lengths = lax.dynamic_slice_in_dim(lengths, side * half_rows_count, half_rows_count, 0)
    query = queries.reshape(half_rows_count, heads_here, head_dim)
    scores = jnp.einsum(
        "rhd,rpd->rhp", query, keys[:, 0], preferred_element_type=f32
    ) * head_dim ** (-0.5)
    position = lax.broadcasted_iota(jnp.int32, (1, 1, span), 2)
    valid = position < own_lengths[:, None, None]
    scores = jnp.where(valid, scores, -1e30)
    peak = jnp.max(scores, axis=-1)
    weights = jnp.where(valid, jnp.exp(scores - peak[..., None]), 0.0)
    total = jnp.sum(weights, axis=-1)
    probs = weights / total[..., None]
    numer = jnp.einsum(
        "rhp,rpd->rhd", probs, values[:, 0].astype(f32), precision=lax.Precision.HIGHEST
    )
    attended_part = numer.astype(jnp.bfloat16).reshape(half_rows_count, heads_here * head_dim)
    attended = lax.all_gather(attended_part, "exp", axis=0, tiled=True)
    cut = out_weight.shape[0]
    own_heads = lax.dynamic_slice_in_dim(attended, side * cut, cut, 1)
    d_model = out_weight.shape[1]
    block = d_model // (n_kvh * n_exp)
    attn_block = (
        lax.psum_scatter(
            lax.dot_general(
                out_weight, own_heads, (((0,), (1,)), ((), ())), preferred_element_type=f32
            ).astype(jnp.bfloat16),
            ("kvh", "exp"),
            scatter_dimension=0,
            tiled=True,
        )
        .astype(jnp.float32)
        .T
    )
    offset = lax.axis_index(("kvh", "exp")) * block
    mixed = lax.dynamic_slice_in_dim(residual, offset, block, 1).astype(f32) + attn_block
    squares = lax.psum(jnp.sum(mixed * mixed, axis=1), ("kvh", "exp"))
    scale = lax.rsqrt(squares / d_model + 1e-06)
    gain_block = lax.dynamic_slice_in_dim(norm_gain, offset, block, 0)
    normed = (mixed * scale[:, None] * gain_block[None, :]).astype(jnp.bfloat16)
    top = expert_ids.shape[1]
    n_slots = replica_map.shape[0]
    n_experts = n_slots // 2
    capacity = min(n_rows, max(2, (3 * n_rows * top + 2 * n_experts - 1) // (2 * n_experts)))
    probs_top = gate_weights / jnp.sum(gate_weights, axis=1, keepdims=True)
    expert_range = jnp.arange(n_experts, dtype=jnp.int32)
    owned = (replica_map[:, None] == expert_range[None, :]).astype(jnp.int32)
    earlier = jnp.cumsum(owned, axis=0) - owned
    rank = jnp.sum(earlier * owned, axis=1)
    copies = jnp.sum(owned, axis=0)
    picked = (expert_ids[..., None] == expert_range).astype(jnp.int32)
    copies_pair = jnp.sum(picked * copies, axis=-1)
    turn = jnp.full((n_rows, top), lax.axis_index("req"), jnp.int32)
    which = turn % copies_pair
    match = (replica_map == expert_ids[..., None]) & (rank == which[..., None])
    slot = jnp.argmax(match, axis=-1)
    mine = slot % n_kvh == lax.axis_index("kvh")
    flat_dest = (slot // n_kvh).reshape(-1)
    flat_mine = mine.reshape(-1)
    toward = (
        (flat_dest[:, None] == jnp.arange(n_req, dtype=jnp.int32)[None, :]) & flat_mine[:, None]
    ).astype(jnp.int32)
    before = jnp.cumsum(toward, axis=0) - toward
    place = jnp.sum(before * toward, axis=1)
    n_buffer = n_req * capacity
    target = jnp.where(flat_mine, flat_dest * capacity + place, n_buffer)
    row_of = jnp.arange(n_rows * top, dtype=jnp.int32) // top
    source = jnp.full((n_buffer,), -1, jnp.int32).at[target].set(row_of, mode="drop")
    half_rows = lax.all_gather(normed.reshape(n_rows, 1, block), "kvh", axis=1, tiled=True).reshape(
        n_rows, n_kvh * block
    )

    def complete(received):
        partner = swapped(received, "exp", 0)
        lead_a = received.shape[0]
        lead_b = received.shape[1]
        own_part = received.reshape(lead_a, lead_b, n_kvh, 1, block)
        other_part = partner.reshape(lead_a, lead_b, n_kvh, 1, block)
        first = jnp.where(side == 0, own_part, other_part)
        second = jnp.where(side == 0, other_part, own_part)
        return jnp.concatenate([first, second], axis=3).reshape(lead_a, lead_b, n_kvh * 2 * block)

    runner = expert_runner(w_gate, w_up, w_down, complete, n_kvh, n_exp, block)
    taken = half_rows[jnp.maximum(source, 0)]
    returned = runner(
        lax.all_to_all(
            jnp.where(source[:, None] >= 0, taken, jnp.zeros((), jnp.bfloat16)).reshape(
                n_req, capacity, half_rows.shape[1]
            ),
            "req",
            split_axis=0,
            concat_axis=0,
            tiled=True,
        )
    )
    flat_back = returned.reshape(n_buffer, n_kvh * block)
    gathered = flat_back[jnp.minimum(target, n_buffer - 1)].reshape(n_rows, top, n_kvh * block)
    weight = jnp.where(mine, probs_top, 0.0)
    partial_value = jnp.zeros((n_rows, n_kvh * block), f32)
    for entry in range(top):
        partial_value = partial_value + weight[:, entry, None] * gathered[:, entry].astype(f32)
    moe_block = (
        lax.psum_scatter(
            partial_value.reshape(n_rows, n_kvh, block).astype(jnp.bfloat16),
            "kvh",
            scatter_dimension=1,
            tiled=True,
        )
        .astype(jnp.float32)
        .reshape(n_rows, block)
    )
    return (mixed + moe_block).astype(jnp.bfloat16)


F32 = jnp.float32
BF16 = jnp.bfloat16
AXES = ("req", "kvh", "exp")
STEP = 16
VMEM_LIMIT = 16 * 2**20


def is_dense(sizes, args):
    queries, keys, expert_ids, replica_map = args[0], args[1], args[7], args[9]
    n_req, n_kvh, n_exp = sizes
    span = keys.shape[2]
    rows = queries.shape[0] // (n_req * n_exp)
    powers = all(size & (size - 1) == 0 for size in (*sizes, span, rows))
    fits = n_req >= 2 and n_kvh >= 2 and n_exp == 2 and rows % (2 * STEP) == 0
    return powers and fits and expert_ids.shape[1] == replica_map.shape[0] // 2


def moved(value, d_req, d_kvh, d_exp):
    n_req, n_kvh, n_exp = (lax.axis_size(axis) for axis in AXES)
    pairs = []
    for req in range(n_req):
        for kvh in range(n_kvh):
            for exp in range(n_exp):
                source = (req * n_kvh + kvh) * n_exp + exp
                target = ((req ^ d_req) * n_kvh + (kvh ^ d_kvh)) * n_exp + (exp ^ d_exp)
                pairs.append((source, target))
    return lax.ppermute(value, AXES, pairs)


def place():
    kvh = lax.axis_index("kvh")
    return lax.axis_index("req"), kvh // 2, kvh % 2, lax.axis_index("exp")


def nt_dot(left, right, **kwargs):
    return lax.dot_general(
        left, right, (((1,), (1,)), ((), ())), preferred_element_type=F32, **kwargs
    )


def nn_dot(left, right):
    return jnp.dot(left, right, preferred_element_type=F32)


def in_vmem(count):
    return [pl.BlockSpec(memory_space=pltpu.VMEM)] * count


def in_smem():
    return pl.BlockSpec(memory_space=pltpu.SMEM)


def called(kernel, args, outs, flops, n_smem=0, scratch=()):
    moves = sum(arg.size * arg.dtype.itemsize for arg in (*args, *outs))
    return pl.pallas_call(
        kernel,
        out_shape=tuple(outs),
        in_specs=[in_smem()] * n_smem + in_vmem(len(args) - n_smem),
        out_specs=tuple(in_vmem(len(outs))),
        scratch_shapes=list(scratch),
        compiler_params=pltpu.CompilerParams(vmem_limit_bytes=VMEM_LIMIT),
        cost_estimate=pl.CostEstimate(flops=flops, bytes_accessed=moves, transcendentals=0),
    )(*args)


def like(shape, dtype):
    return jax.ShapeDtypeStruct(shape, dtype)


def attention_kernel(chips, lengths, query, key, value, weight, down, *refs):
    blocks, weight_copy, pieces = refs[:4], refs[4], refs[5:-5]
    limits, rows_ref, key_ref, value_ref, sems = refs[-5:]
    _, _, core, side = place()
    n_rows = query.shape[0]
    span, head_dim = key.shape[2], key.shape[3]
    heads = query.shape[1] // head_dim
    n = STEP
    steps = n_rows // n
    half = steps // 2

    def cached(step, index):
        source, target = ((key, key_ref), (value, value_ref))[index]
        here = pl.ds(step * n, n)
        return pltpu.make_async_copy(source.at[here], target.at[here], sems.at[2 * step + index])

    begin = [
        pltpu.make_async_copy(query, rows_ref, sems.at[2 * steps]),
        pltpu.make_async_copy(lengths, limits, sems.at[2 * steps + 1]),
    ]
    rest = [pltpu.make_async_copy(weight, weight_copy, sems.at[2 * steps + 2])]
    block = pieces[0].shape[1] // 2
    for piece, (d_exp, d_row) in zip(pieces, chips, strict=True):
        for index in range(2):
            source = down.at[0, :, pl.ds(columns_of(d_exp, d_row, index, block), block)]
            target = piece.at[:, index * block : (index + 1) * block]
            sem = sems.at[2 * steps + 2 + len(rest)]
            rest.append(pltpu.make_async_copy(source, target, sem))
    for copy in begin:
        copy.start()
    for step in range(steps):
        for index in range(2):
            cached(step, index).start()
    for copy in rest:
        copy.start()
    column = lax.broadcasted_iota(jnp.int32, (1, n * span), 1)
    owner = lax.shift_right_logical(column, span.bit_length() - 1)
    position = column & (span - 1)
    request = lax.broadcasted_iota(jnp.int32, (heads * n, 1), 0) & (n - 1)
    same = request == owner
    for copy in begin:
        copy.wait()

    @pl.loop(0, steps)
    def _(step):
        here = pl.ds(pl.multiple_of(step * n, n), n)
        rows = jnp.concatenate(
            [rows_ref[here, head * head_dim : (head + 1) * head_dim] for head in range(heads)],
            axis=0,
        )
        limit = jnp.zeros((1, n * span), jnp.int32)
        first = side * n_rows + step * n
        for index in range(n):
            limit = jnp.where(owner == index, limits[first + index], limit)
        valid = same & (position < limit)
        cached(step, 0).wait()
        scores = nt_dot(rows, key_ref[here].reshape(n * span, head_dim)) * head_dim ** (-0.5)
        scores = jnp.where(valid, scores, -1e30)
        peak = jnp.max(scores, axis=1, keepdims=True)
        weights = jnp.exp(scores - peak)
        total = jnp.sum(weights, axis=1, keepdims=True)
        high = weights.astype(BF16)
        low = (weights - high.astype(F32)).astype(BF16)
        cached(step, 1).wait()
        held = value_ref[here].reshape(n * span, head_dim)
        both = nn_dot(jnp.concatenate([high, low], axis=0), held)
        numer = (both[: heads * n] + both[heads * n :]) / total
        by_head = [numer[head * n : (head + 1) * n].astype(BF16) for head in range(heads)]
        lower = jnp.concatenate(by_head[: heads // 2], axis=1)
        upper = jnp.concatenate(by_head[heads // 2 :], axis=1)
        near = jnp.where(side == 0, lower, upper)
        far = jnp.where(side == 0, upper, lower)
        passed = step >= half
        spot = pl.ds(pl.multiple_of((step - jnp.where(passed, half, 0)) * n, n), n)
        at_home = passed == (core == 1)

        @pl.when(at_home)
        def _():
            blocks[0][spot, :] = near
            blocks[1][spot, :] = far

        @pl.when(jnp.logical_not(at_home))
        def _():
            blocks[2][spot, :] = near
            blocks[3][spot, :] = far

    for copy in rest:
        copy.wait()


def attention(chips, queries, keys, values, lengths, out_weight, w_down, block):
    rows = queries.shape[0]
    span = keys.shape[2]
    piece = like((rows // 2, queries.shape[1] // 2), BF16)
    args = (lengths, queries, keys, values, out_weight, w_down)
    outs = [piece] * 4 + [like(out_weight.shape, BF16)]
    outs += [like((w_down.shape[1], 2 * block), BF16)] * len(chips)
    return pl.pallas_call(
        lambda *refs: attention_kernel(chips, *refs),
        out_shape=tuple(outs),
        in_specs=[pl.BlockSpec(memory_space=pltpu.HBM)] * len(args),
        out_specs=tuple(in_vmem(len(outs))),
        scratch_shapes=[
            pltpu.SMEM(lengths.shape, jnp.int32),
            pltpu.VMEM(queries.shape, BF16),
            pltpu.VMEM(keys.shape, BF16),
            pltpu.VMEM(values.shape, BF16),
            pltpu.SemaphoreType.DMA((3 + 2 * (rows // STEP) + 2 * len(chips),)),
        ],
        cost_estimate=pl.CostEstimate(
            flops=6 * STEP * rows * queries.shape[1] * span,
            bytes_accessed=2 * keys.size * 2,
            transcendentals=0,
        ),
        compiler_params=pltpu.CompilerParams(vmem_limit_bytes=VMEM_LIMIT),
        name="attention",
    )(*(pltpu.with_memory_space_constraint(arg, pltpu.HBM) for arg in args))


def routes_kernel(slots, ids, gates, shares, serves):
    probs_top = gates[...] / jnp.sum(gates[...], axis=0, keepdims=True)
    n_experts = shares.shape[0]
    for expert in range(n_experts):
        shares[expert : expert + 1, :] = jnp.sum(
            jnp.where(ids[...] == expert, probs_top, 0.0), axis=0, keepdims=True
        )
    req, row, core, _ = place()
    n_kvh = lax.axis_size("kvh")
    lane = lax.broadcasted_iota(jnp.int32, (1, n_experts), 1)
    n_req = serves.shape[0] // 2
    for index, at in enumerate((core, 1 - core)):
        slot = req * n_kvh + row * 2 + at
        expert = slots[slot]
        copies = jnp.int32(0)
        rank = jnp.int32(0)
        for other in range(slots.shape[0]):
            same = (slots[other] == expert).astype(jnp.int32)
            copies = copies + same
            rank = rank + jnp.where(other < slot, same, 0)
        for d_req in range(n_req):
            chosen = jnp.where(lax.rem(req ^ d_req, copies) == rank, expert, -1)
            serves[2 * d_req + index : 2 * d_req + index + 1, :] = (lane == chosen).astype(F32)


def columns_of(d_exp, d_row, index, block):
    _, row, _, side = place()
    return pl.multiple_of((((row ^ d_row) * 2 + index) * 2 + (side ^ d_exp)) * block, block)


def projection_kernel(chips, *refs):
    pieces, (near_weight, far_weight, residual), outs = refs[:4], refs[4:7], refs[7:-2]
    near, far = refs[-2:]
    _, _, core, side = place()
    rows = pieces[0].shape[0]
    block = outs[0].shape[1] // 2
    spots = [pl.ds(pl.multiple_of((side ^ d) * rows, rows), rows) for d in range(2)]
    for d in range(2):
        near[spots[d], :] = pieces[d][...]
        far[spots[d], :] = pieces[2 + d][...]
    for chip, (d_exp, d_row) in enumerate(chips):
        for index in range(2):
            start = columns_of(d_exp, d_row, index, block)
            where = pl.ds(start, block)
            part = nn_dot(near[...], near_weight[:, where]) + nn_dot(far[...], far_weight[:, where])
            here = slice(index * block, (index + 1) * block)
            if chip:
                outs[chip][:, here] = part.astype(BF16)
                continue
            for half in range(2):
                own = slice(half * rows, (half + 1) * rows)
                at = pl.ds(pl.multiple_of((half * 2 + core) * rows, rows), rows)
                outs[0][own, here] = part[own] + residual[at, where].astype(F32)


def own_tokens(rows, n_tokens, core):
    half = rows // 2
    local = lax.broadcasted_iota(jnp.int32, (rows, 1), 0)
    token = local + jnp.where(local >= half, half, 0) + core * half
    lane = lax.broadcasted_iota(jnp.int32, (rows, n_tokens), 1)
    return (lane == token).astype(F32)


def mixed_kernel(count, *refs):
    own, others, (gain, shares, mixed, sent) = refs[0], refs[1:count], refs[count:]
    rows = own.shape[0]
    block = own.shape[1] // 2
    _, _, core, _ = place()
    for index in range(2):
        here = slice(index * block, (index + 1) * block)
        total = own[:, here]
        for other in others:
            total = total + other[:, here].astype(F32)
        mixed[:, here] = total
        scale = gain[:, pl.ds(columns_of(0, 0, index, block), block)]
        sent[:rows, here] = (total * scale).astype(BF16)
    chosen = own_tokens(rows, shares.shape[1], core)
    table = nt_dot(shares[...], chosen, precision=lax.Precision.HIGHEST)
    high = table.astype(BF16)
    low = (table - high.astype(F32)).astype(BF16)
    rest = jnp.zeros((table.shape[0], 2 * block - 2 * rows), BF16)
    sent[rows:, :] = jnp.concatenate([high, low, rest], axis=1)


def joined_kernel(*refs):
    out = refs[-1]
    rows = out.shape[0] // (len(refs) - 1)
    for index, ref in enumerate(refs[:-1]):
        out[index * rows : (index + 1) * rows, :] = ref[:rows, :]


def expert_kernel(chips, groups, *refs):
    serves, gain = refs[0], refs[1]
    weights = refs[2:6]
    sents = refs[6 : 6 + len(groups)]
    parts = refs[6 + len(groups) : -1]
    act_ref = refs[-1]
    rows = parts[0].shape[0] // len(groups)
    block = parts[0].shape[1] // 2
    hidden, d_model = weights[0].shape
    gates = None
    squares = None
    for part_ref, (d_exp, d_row) in zip(parts, chips, strict=True):
        for index in range(2):
            where = pl.ds(columns_of(d_exp, d_row, index, block), block)
            part = part_ref[:, index * block : (index + 1) * block]
            weight = jnp.concatenate([ref[:, where] for ref in weights], axis=0)
            product = nt_dot(part, weight)
            plain = part.astype(F32) / gain[:, where]
            square = jnp.sum(plain * plain, axis=1, keepdims=True)
            gates = product if gates is None else gates + product
            squares = square if squares is None else squares + square
    scale = lax.rsqrt(squares / d_model + 1e-06)
    gate = gates[:, : 2 * hidden] * scale
    up = gates[:, 2 * hidden :] * scale
    act = gate / (1.0 + jnp.exp(-gate)) * up
    lane = lax.broadcasted_iota(jnp.int32, (rows, 2 * rows), 1)
    local = lax.broadcasted_iota(jnp.int32, (rows, 2 * rows), 0)
    chosen = ((lane == local) | (lane == local + rows)).astype(BF16)
    factors = []
    for sent, d_req in zip(sents, groups, strict=True):
        table = nt_dot(chosen, sent[rows:, : 2 * rows])
        factors.append(
            [
                jnp.sum(table * serves[row : row + 1, :], axis=1, keepdims=True)
                for row in (2 * d_req, 2 * d_req + 1)
            ]
        )
    first = jnp.concatenate([pair[0] for pair in factors], axis=0)
    second = jnp.concatenate([pair[1] for pair in factors], axis=0)
    unit = lax.broadcasted_iota(jnp.int32, act.shape, 1)
    act_ref[...] = (act * jnp.where(unit < hidden, first, second)).astype(BF16)


def combine_kernel(count, groups, *refs):
    acts, near, far = refs[:count], refs[count : 2 * count], refs[2 * count : 3 * count]
    rest = refs[3 * count :]
    mixed = None
    if 0 in groups:
        mixed, rest = rest[0], rest[1:]
    rows = acts[0].shape[0] // len(groups)
    total = None
    for act, low, high in zip(acts, near, far, strict=True):
        product = nn_dot(act[...], jnp.concatenate([low[...], high[...]], axis=0))
        total = product if total is None else total + product
    for index, (d_req, out) in enumerate(zip(groups, rest, strict=True)):
        part = total[index * rows : (index + 1) * rows]
        if d_req == 0:
            part = part + mixed[...]
        out[...] = part.astype(out.dtype)


def summed_kernel(*refs):
    terms, (own_out, other_out) = refs[:-2], refs[-2:]
    _, _, core, _ = place()
    total = terms[0][...]
    for term in terms[1:]:
        total = total + term[...].astype(F32)
    block = total.shape[1] // 2
    own_out[...] = jnp.where(core == 0, total[:, :block], total[:, block:]).astype(BF16)
    other_out[...] = jnp.where(core == 0, total[:, block:], total[:, :block]).astype(BF16)


def final_kernel(own, other, out):
    _, _, core, _ = place()
    rows = own.shape[0] // 2
    for part, place_of in ((own, core), (other, 1 - core)):
        for half in range(2):
            at = pl.ds(pl.multiple_of((half * 2 + place_of) * rows, rows), rows)
            out[at, :] = part[half * rows : (half + 1) * rows, :]


def exchanged(parts, chips):
    return [
        moved(part, 0, 2 * d_row, d_exp) if d_exp or d_row else part
        for part, (d_exp, d_row) in zip(parts, chips, strict=True)
    ]


def spread(value, chips):
    return exchanged([value] * len(chips), chips)


def dense_shards(*args):
    return dense_layer(*args)


def dense_layer(
    queries,
    keys,
    values,
    lengths,
    out_weight,
    residual,
    norm_gain,
    expert_ids,
    gate_weights,
    replica_map,
    w_gate,
    w_up,
    w_down,
):
    n_req, n_kvh, n_exp = (lax.axis_size(axis) for axis in AXES)
    d_model = out_weight.shape[1]
    block = d_model // (n_kvh * n_exp)
    rows = queries.shape[0]
    n_experts = expert_ids.shape[1]
    hidden = w_gate.shape[2]
    chips = [(d_exp, d_row) for d_row in range(n_kvh // 2) for d_exp in range(n_exp)]
    n_chips = len(chips)
    gain = norm_gain.reshape(1, d_model)

    blocks = attention(chips, queries, keys, values, lengths, out_weight, w_down, block)
    down, near_weight, blocks = blocks[5:], blocks[4], list(blocks[:4])
    shares, serves = called(
        routes_kernel,
        (replica_map, expert_ids.T, gate_weights.T),
        [like((n_experts, expert_ids.shape[0]), F32), like((2 * n_req, n_experts), F32)],
        flops=0,
        n_smem=1,
    )
    blocks[3] = moved(blocks[3], 0, 1, 1)
    blocks[1] = moved(blocks[1], 0, 0, 1)
    far_weight = moved(near_weight, 0, 1, 0)
    blocks[2] = moved(blocks[2], 0, 1, 0)
    blocks[3], serves, shares = lax.optimization_barrier((blocks[3], serves, shares))
    wide = (rows, 2 * block)
    sums = called(
        lambda *refs: projection_kernel(chips, *refs),
        (*blocks, near_weight, far_weight, residual),
        [like(wide, F32)] + [like(wide, BF16)] * (n_chips - 1),
        flops=4 * rows * out_weight.size,
        scratch=[pltpu.VMEM((rows, blocks[0].shape[1]), BF16)] * 2,
    )
    w_in = [w_gate[0].T, w_up[0].T]
    later, _ = lax.optimization_barrier((tuple(w_in), sums[1]))
    w_in = [w_in[0], moved(later[0], 0, 1, 0), w_in[1], moved(later[1], 0, 1, 0)]
    down, _ = lax.optimization_barrier((tuple(down), sums[1]))
    sums = exchanged(sums, chips)
    down = exchanged(down, chips)
    down_far = [moved(piece, 0, 1, 0) for piece in down]
    mixed, sent = called(
        lambda *refs: mixed_kernel(n_chips, *refs),
        (*sums, gain, shares),
        [like(wide, F32), like((rows + n_experts, 2 * block), BF16)],
        flops=8 * rows * block,
    )
    order = range(1, n_req)
    by_group = {0: sent, **{d_req: moved(sent, d_req, 0, 0) for d_req in order}}
    half = n_req // 2
    order = [0, *order]
    terms = {}
    for groups in (tuple(order[:half]), tuple(order[half:])):
        (joined,) = called(
            joined_kernel,
            [by_group[d_req] for d_req in groups],
            [like((half * rows, 2 * block), BF16)],
            flops=0,
        )
        parts = spread(joined, chips)
        (act,) = called(
            lambda *refs, groups=groups: expert_kernel(chips, groups, *refs),
            (serves, gain, *w_in, *(by_group[d_req] for d_req in groups), *parts),
            [like((half * rows, 2 * hidden), BF16)],
            flops=8 * half * rows * d_model * hidden,
        )
        tail = (mixed,) if 0 in groups else ()
        results = called(
            lambda *refs, groups=groups: combine_kernel(n_chips, groups, *refs),
            (*spread(act, chips), *down, *down_far, *tail),
            [like(wide, F32 if d_req == 0 else BF16) for d_req in groups],
            flops=8 * half * rows * hidden * n_chips * block,
        )
        for d_req, result in zip(groups, results, strict=True):
            terms[d_req] = moved(result, d_req, 0, 0) if d_req else result
    own, other = called(
        summed_kernel,
        [terms[d_req] for d_req in order],
        [like((rows, block), BF16)] * 2,
        flops=4 * n_req * rows * block,
    )
    (out,) = called(
        final_kernel,
        (own, moved(other, 0, 1, 0)),
        [like((2 * rows, block), BF16)],
        flops=4 * rows * block,
    )
    return out


def solution(mesh):
    in_specs = (
        P(("req", "exp"), "kvh"),
        P(("req", "exp"), "kvh", None, None),
        P(("req", "exp"), "kvh", None, None),
        P("req"),
        P(("kvh", "exp"), None),
        P("req", None),
        P(),
        P("req", None),
        P("req", None),
        P(),
        P(("req", "kvh"), None, "exp"),
        P(("req", "kvh"), None, "exp"),
        P(("req", "kvh"), "exp", None),
    )
    out_specs = P("req", ("kvh", "exp"))
    sizes = tuple(mesh.shape[axis] for axis in AXES)

    def run(*args):
        dense = is_dense(sizes, args)
        step = jax.shard_map(
            dense_shards if dense else routed_shards,
            mesh=mesh,
            in_specs=in_specs,
            out_specs=out_specs,
            check_vma=False,
        )
        return step(*args)

    return run
```

profile of v0, /device:TPU:0, one launch (start us, length us, event | category | flops | bytes accessed | tf_op | source)
XLA Modules:
  0.0 80.4 jit_solution(4494273610000361373)
XLA Ops:
  0.0 3.8 %attention.1 = (bf16[32,256]{1,0:T(8,128)(2,1)S(1)}, bf16[32,256]{1,0:T(8,128)(2,1)S(1)}, bf16[32,256]{1,0:T(8,128)(2,1)S(1)}, bf16[32,256]{1,0:T(8,128)(2,1)S(1...) custom-call(s32[128]{0:T(128)} %refs_0_.1, ...), custom_call_target="tpu_custom_call" | custom-call | flops 201326592 | bytes 2097152 | tf_op jit(solution)/shard_map/attention/pallas_call | solution.py:341
  3.8 0.6 collective-permute-start.3
  4.3 2.6 %collective-permute-start = (bf16[32,256]{1,0:T(8,128)(2,1)S(1)}, bf16[32,256]{1,0:T(8,128)(2,1)S(1)}, u32[]{:S(2)}, u32[]{:S(2)}) collective-permute-start(bf16[32,256]{1,0:T(8,128)(2,1)S(1)} %get-tuple-element.37), channel_id=1, source_target_pairs={{0,3},{1,2},{2,1},{3,0},{4,7},{5,6},{6,5},{7,4},{8,11},{9,10},{10,... | collective-permute-start | bytes 49160 | tf_op jit(solution)/shard_map/ppermute | solution.py:201
  7.1 0.6 copy-done.6
  7.7 0.6 shard_map.127
  8.4 2.3 %collective-permute-done.1.refs_1_ = bf16[32,256]{1,0:T(8,128)(2,1)S(1)} collective-permute-done((bf16[32,256]{1,0:T(8,128)(2,1)S(1)}, bf16[32,256]{1,0:T(8,128)(2,1)S(1)}, u32[]{:S(2)}, u32[]{:S(2)}) %collective-permute-start.1) | collective-permute-done | bytes 16416 | tf_op jit(solution)/shard_map/ppermute | solution.py:201
  10.7 0.5 shard_map.128
  11.2 0.6 copy-done
  12.5 1.9 %collective-permute-start.7 = (bf16[64,512]{1,0:T(8,128)(2,1)S(1)}, bf16[64,512]{1,0:T(8,128)(2,1)S(1)}, u32[]{:S(2)}, u32[]{:S(2)}) collective-permute-start(bf16[64,512]{1,0:T(8,128)(2,1)S(1)} %get-tuple-element.50), channel_id=1, source_target_pairs={{0,4},{1,5},{2,6},{3,7},{4,0},{5,1},{6,2},{7,3},{8,12},{9,13},{10,... | collective-permute-start | bytes 196616 | tf_op jit(solution)/shard_map/ppermute | solution.py:201
  14.4 1.4 %collective-permute-start.8 = (bf16[64,512]{1,0:T(8,128)(2,1)S(1)}, bf16[64,512]{1,0:T(8,128)(2,1)S(1)}, u32[]{:S(2)}, u32[]{:S(2)}) collective-permute-start(bf16[64,512]{1,0:T(8,128)(2,1)S(1)} %get-tuple-element.51), channel_id=1, source_target_pairs={{0,5},{1,4},{2,7},{3,6},{4,1},{5,0},{6,3},{7,2},{8,13},{9,12},{10,... | collective-permute-start | bytes 196616 | tf_op jit(solution)/shard_map/ppermute | solution.py:201
  15.8 1.0 %collective-permute-done.6.refs_1_ = bf16[64,512]{1,0:T(8,128)(2,1)S(1)} collective-permute-done((bf16[64,512]{1,0:T(8,128)(2,1)S(1)}, bf16[64,512]{1,0:T(8,128)(2,1)S(1)}, u32[]{:S(2)}, u32[]{:S(2)}) %collective-permute-start.6) | collective-permute-done | bytes 65568 | tf_op jit(solution)/shard_map/ppermute | solution.py:201
  16.9 0.7 collective-permute-done.7.refs_2_
  17.6 2.3 %collective-permute-done.8.refs_3_ = bf16[64,512]{1,0:T(8,128)(2,1)S(1)} collective-permute-done((bf16[64,512]{1,0:T(8,128)(2,1)S(1)}, bf16[64,512]{1,0:T(8,128)(2,1)S(1)}, u32[]{:S(2)}, u32[]{:S(2)}) %collective-permute-start.8) | collective-permute-done | bytes 65568 | tf_op jit(solution)/shard_map/ppermute | solution.py:201
  20.1 1.6 %collective-permute-start.9 = (bf16[72,512]{1,0:T(8,128)(2,1)S(1)}, bf16[72,512]{1,0:T(8,128)(2,1)S(1)}, u32[]{:S(2)}, u32[]{:S(2)}) collective-permute-start(bf16[72,512]{1,0:T(8,128)(2,1)S(1)} %get-tuple-element.53.refs_0_.refs_6_), channel_id=1, source_target_pairs={{0,8},{1,9},{2,10},{3,11},{4,12},{5,13},{6,14},{7,15},{8,0},{9,1},... | collective-permute-start | bytes 221192 | tf_op jit(solution)/shard_map/ppermute | solution.py:201
  21.7 2.6 %collective-permute-start.24 = (bf16[72,512]{1,0:T(8,128)(2,1)S(1)}, bf16[72,512]{1,0:T(8,128)(2,1)S(1)}, u32[]{:S(2)}, u32[]{:S(2)}) collective-permute-start(bf16[72,512]{1,0:T(8,128)(2,1)S(1)} %get-tuple-element.53.refs_0_.refs_6_), channel_id=1, source_target_pairs={{0,16},{1,17},{2,18},{3,19},{4,20},{5,21},{6,22},{7,23},{8,24},{9,... | collective-permute-start | bytes 221192 | tf_op jit(solution)/shard_map/ppermute | solution.py:201
  24.3 0.3 collective-permute-done.9.refs_1_.refs_7_
  24.7 0.6 collective-permute-start.17
  25.3 2.7 %collective-permute-done.24.refs_0_.refs_6_ = bf16[72,512]{1,0:T(8,128)(2,1)S(1)} collective-permute-done((bf16[72,512]{1,0:T(8,128)(2,1)S(1)}, bf16[72,512]{1,0:T(8,128)(2,1)S(1)}, u32[]{:S(2)}, u32[]{:S(2)}) %collective-permute-start.24) | collective-permute-done | bytes 73760 | tf_op jit(solution)/shard_map/ppermute | solution.py:201
  28.0 1.4 %collective-permute-start.25 = (bf16[72,512]{1,0:T(8,128)(2,1)S(1)}, bf16[72,512]{1,0:T(8,128)(2,1)S(1)}, u32[]{:S(2)}, u32[]{:S(2)}) collective-permute-start(bf16[72,512]{1,0:T(8,128)(2,1)S(1)} %get-tuple-element.53.refs_0_.refs_6_), channel_id=1, source_target_pairs={{0,24},{1,25},{2,26},{3,27},{4,28},{5,29},{6,30},{7,31},{8,16},{9,... | collective-permute-start | bytes 221192 | tf_op jit(solution)/shard_map/ppermute | solution.py:201
  29.5 4.7 %collective-permute-done.25.refs_1_.refs_7_ = bf16[72,512]{1,0:T(8,128)(2,1)S(1)} collective-permute-done((bf16[72,512]{1,0:T(8,128)(2,1)S(1)}, bf16[72,512]{1,0:T(8,128)(2,1)S(1)}, u32[]{:S(2)}, u32[]{:S(2)}) %collective-permute-start.25) | collective-permute-done | bytes 73760 | tf_op jit(solution)/shard_map/ppermute | solution.py:201
  34.2 1.9 %collective-permute-start.18 = (bf16[192,512]{1,0:T(8,128)(2,1)S(1)}, bf16[192,512]{1,0:T(8,128)(2,1)S(1)}, u32[]{:S(2)}, u32[]{:S(2)}) collective-permute-start(bf16[192,512]{1,0:T(8,128)(2,1)S(1)} %get-tuple-element.61), channel_id=1, source_target_pairs={{0,5},{1,4},{2,7},{3,6},{4,1},{5,0},{6,3},{7,2},{8,13},{9,12},{10,... | collective-permute-start | bytes 589832 | tf_op jit(solution)/shard_map/ppermute | solution.py:201
  36.3 5.2 %collective-permute-done.18.refs_7_ = bf16[192,512]{1,0:T(8,128)(2,1)S(1)} collective-permute-done((bf16[192,512]{1,0:T(8,128)(2,1)S(1)}, bf16[192,512]{1,0:T(8,128)(2,1)S(1)}, u32[]{:S(2)}, u32[]{:S(2)}) %collective-permute-start.18) | collective-permute-done | bytes 196640 | tf_op jit(solution)/shard_map/ppermute | solution.py:201
  41.4 1.5 %collective-permute-start.11 = (bf16[128,512]{1,0:T(8,128)(2,1)S(1)}, bf16[128,512]{1,0:T(8,128)(2,1)S(1)}, u32[]{:S(2)}, u32[]{:S(2)}) collective-permute-start(bf16[128,512]{1,0:T(8,128)(2,1)S(1)} %shard_map.130.refs_8_), channel_id=1, source_target_pairs={{0,4},{1,5},{2,6},{3,7},{4,0},{5,1},{6,2},{7,3},{8,12},{9,13},{10,... | collective-permute-start | bytes 393224 | tf_op jit(solution)/shard_map/ppermute | solution.py:201
  43.0 3.4 %collective-permute-start.12 = (bf16[128,512]{1,0:T(8,128)(2,1)S(1)}, bf16[128,512]{1,0:T(8,128)(2,1)S(1)}, u32[]{:S(2)}, u32[]{:S(2)}) collective-permute-start(bf16[128,512]{1,0:T(8,128)(2,1)S(1)} %shard_map.130.refs_8_), channel_id=1, source_target_pairs={{0,5},{1,4},{2,7},{3,6},{4,1},{5,0},{6,3},{7,2},{8,13},{9,12},{10,... | collective-permute-start | bytes 393224 | tf_op jit(solution)/shard_map/ppermute | solution.py:201
  46.7 2.6 %collective-permute-done.12.refs_11_ = bf16[128,512]{1,0:T(8,128)(2,1)S(1)} collective-permute-done((bf16[128,512]{1,0:T(8,128)(2,1)S(1)}, bf16[128,512]{1,0:T(8,128)(2,1)S(1)}, u32[]{:S(2)}, u32[]{:S(2)}) %collective-permute-start.12) | collective-permute-done | bytes 131104 | tf_op jit(solution)/shard_map/ppermute | solution.py:201
  49.3 0.5 collective-permute-start.27
  49.8 1.6 %collective-permute-done.26.refs_9_ = bf16[128,512]{1,0:T(8,128)(2,1)S(1)} collective-permute-done((bf16[128,512]{1,0:T(8,128)(2,1)S(1)}, bf16[128,512]{1,0:T(8,128)(2,1)S(1)}, u32[]{:S(2)}, u32[]{:S(2)}) %collective-permute-start.26) | collective-permute-done | bytes 131104 | tf_op jit(solution)/shard_map/ppermute | solution.py:201
  51.5 0.5 collective-permute-start.22
  52.0 1.3 %collective-permute-start.28 = (bf16[128,512]{1,0:T(8,128)(2,1)S(1)}, bf16[128,512]{1,0:T(8,128)(2,1)S(1)}, u32[]{:S(2)}, u32[]{:S(2)}) collective-permute-start(bf16[128,512]{1,0:T(8,128)(2,1)S(1)} %shard_map.133.refs_8_), channel_id=1, source_target_pairs={{0,5},{1,4},{2,7},{3,6},{4,1},{5,0},{6,3},{7,2},{8,13},{9,12},{10,... | collective-permute-start | bytes 393224 | tf_op jit(solution)/shard_map/ppermute | solution.py:201
  53.3 1.4 %shard_map.131.refs_0_ = bf16[128,384]{1,0:T(8,128)(2,1)S(1)} custom-call(f32[8,8]{1,0:T(8,128)S(1)} %get-tuple-element.40.refs_0_, f32[1,2048]{1,0:T(1,128)S(1)} %bitcast.16, bf16[192,2048]{1,0:T(8,128)(2,1)S(1)} %bitcast.10, bf16[192,2048]{1,0:T(8,128)(2,1)S(1)} %collective-permute-done.4.refs_3_, bf16[192,2048]{1,0:T(8,128)(2,1)S(1)} %bitcast.13, ...), custom_call_target="tpu_custom_call" | custom-call | flops 402653184 | bytes 3924224 | tf_op jit(solution)/shard_map/pallas_call | solution.py:229
  54.7 2.7 %collective-permute-start.13 = (bf16[128,384]{1,0:T(8,128)(2,1)S(1)}, bf16[128,384]{1,0:T(8,128)(2,1)S(1)}, u32[]{:S(2)}, u32[]{:S(2)}) collective-permute-start(bf16[128,384]{1,0:T(8,128)(2,1)S(1)} %shard_map.131.refs_0_), channel_id=1, source_target_pairs={{0,1},{1,0},{2,3},{3,2},{4,5},{5,4},{6,7},{7,6},{8,9},{9,8},{10,11... | collective-permute-start | bytes 294920 | tf_op jit(solution)/shard_map/ppermute | solution.py:201
  57.4 1.2 %collective-permute-done.28.refs_11_ = bf16[128,512]{1,0:T(8,128)(2,1)S(1)} collective-permute-done((bf16[128,512]{1,0:T(8,128)(2,1)S(1)}, bf16[128,512]{1,0:T(8,128)(2,1)S(1)}, u32[]{:S(2)}, u32[]{:S(2)}) %collective-permute-start.28) | collective-permute-done | bytes 131104 | tf_op jit(solution)/shard_map/ppermute | solution.py:201
  58.6 1.4 %collective-permute-start.14 = (bf16[128,384]{1,0:T(8,128)(2,1)S(1)}, bf16[128,384]{1,0:T(8,128)(2,1)S(1)}, u32[]{:S(2)}, u32[]{:S(2)}) collective-permute-start(bf16[128,384]{1,0:T(8,128)(2,1)S(1)} %shard_map.131.refs_0_), channel_id=1, source_target_pairs={{0,4},{1,5},{2,6},{3,7},{4,0},{5,1},{6,2},{7,3},{8,12},{9,13},{10,... | collective-permute-start | bytes 294920 | tf_op jit(solution)/shard_map/ppermute | solution.py:201
  60.0 2.0 %collective-permute-start.15 = (bf16[128,384]{1,0:T(8,128)(2,1)S(1)}, bf16[128,384]{1,0:T(8,128)(2,1)S(1)}, u32[]{:S(2)}, u32[]{:S(2)}) collective-permute-start(bf16[128,384]{1,0:T(8,128)(2,1)S(1)} %shard_map.131.refs_0_), channel_id=1, source_target_pairs={{0,5},{1,4},{2,7},{3,6},{4,1},{5,0},{6,3},{7,2},{8,13},{9,12},{10,... | collective-permute-start | bytes 294920 | tf_op jit(solution)/shard_map/ppermute | solution.py:201
  62.1 1.4 %shard_map.134.refs_0_ = bf16[128,384]{1,0:T(8,128)(2,1)S(1)} custom-call(f32[8,8]{1,0:T(8,128)S(1)} %get-tuple-element.40.refs_0_, f32[1,2048]{1,0:T(1,128)S(1)} %bitcast.17, bf16[192,2048]{1,0:T(8,128)(2,1)S(1)} %bitcast.11, bf16[192,2048]{1,0:T(8,128)(2,1)S(1)} %collective-permute-done.4.refs_3_, bf16[192,2048]{1,0:T(8,128)(2,1)S(1)} %bitcast.14, ...), custom_call_target="tpu_custom_call" | custom-call | flops 402653184 | bytes 3924224 | tf_op jit(solution)/shard_map/pallas_call | solution.py:229
  63.6 1.4 %collective-permute-start.30 = (bf16[128,384]{1,0:T(8,128)(2,1)S(1)}, bf16[128,384]{1,0:T(8,128)(2,1)S(1)}, u32[]{:S(2)}, u32[]{:S(2)}) collective-permute-start(bf16[128,384]{1,0:T(8,128)(2,1)S(1)} %shard_map.134.refs_0_), channel_id=1, source_target_pairs={{0,4},{1,5},{2,6},{3,7},{4,0},{5,1},{6,2},{7,3},{8,12},{9,13},{10,... | collective-permute-start | bytes 294920 | tf_op jit(solution)/shard_map/ppermute | solution.py:201
  65.0 2.0 %collective-permute-start.31 = (bf16[128,384]{1,0:T(8,128)(2,1)S(1)}, bf16[128,384]{1,0:T(8,128)(2,1)S(1)}, u32[]{:S(2)}, u32[]{:S(2)}) collective-permute-start(bf16[128,384]{1,0:T(8,128)(2,1)S(1)} %shard_map.134.refs_0_), channel_id=1, source_target_pairs={{0,5},{1,4},{2,7},{3,6},{4,1},{5,0},{6,3},{7,2},{8,13},{9,12},{10,... | collective-permute-start | bytes 294920 | tf_op jit(solution)/shard_map/ppermute | solution.py:201
  67.0 0.4 shard_map.132
  67.6 0.6 collective-permute-done.29.refs_1_
  68.2 0.3 collective-permute-done.30.refs_2_
  68.5 2.0 %collective-permute-done.31.refs_3_ = bf16[128,384]{1,0:T(8,128)(2,1)S(1)} collective-permute-done((bf16[128,384]{1,0:T(8,128)(2,1)S(1)}, bf16[128,384]{1,0:T(8,128)(2,1)S(1)}, u32[]{:S(2)}, u32[]{:S(2)}) %collective-permute-start.31) | collective-permute-done | bytes 98336 | tf_op jit(solution)/shard_map/ppermute | solution.py:201
  70.5 0.4 shard_map.135
  71.0 1.4 %collective-permute-start.32 = (bf16[64,512]{1,0:T(8,128)(2,1)S(1)}, bf16[64,512]{1,0:T(8,128)(2,1)S(1)}, u32[]{:S(2)}, u32[]{:S(2)}) collective-permute-start(bf16[64,512]{1,0:T(8,128)(2,1)S(1)} %get-tuple-element.65), channel_id=1, source_target_pairs={{0,16},{1,17},{2,18},{3,19},{4,20},{5,21},{6,22},{7,23},{8,24},{9,... | collective-permute-start | bytes 196616 | tf_op jit(solution)/shard_map/ppermute | solution.py:201
  72.4 0.5 collective-permute-start.33
  72.9 3.3 %collective-permute-done.32.refs_2_ = bf16[64,512]{1,0:T(8,128)(2,1)S(1)} collective-permute-done((bf16[64,512]{1,0:T(8,128)(2,1)S(1)}, bf16[64,512]{1,0:T(8,128)(2,1)S(1)}, u32[]{:S(2)}, u32[]{:S(2)}) %collective-permute-start.32) | collective-permute-done | bytes 65568 | tf_op jit(solution)/shard_map/ppermute | solution.py:201
  76.2 2.2 %collective-permute-done.33.refs_3_ = bf16[64,512]{1,0:T(8,128)(2,1)S(1)} collective-permute-done((bf16[64,512]{1,0:T(8,128)(2,1)S(1)}, bf16[64,512]{1,0:T(8,128)(2,1)S(1)}, u32[]{:S(2)}, u32[]{:S(2)}) %collective-permute-start.33) | collective-permute-done | bytes 65568 | tf_op jit(solution)/shard_map/ppermute | solution.py:201
  78.5 1.2 %collective-permute-done.34.other = bf16[64,256]{1,0:T(8,128)(2,1)S(1)} collective-permute-done((bf16[64,256]{1,0:T(8,128)(2,1)S(1)}, bf16[64,256]{1,0:T(8,128)(2,1)S(1)}, u32[]{:S(2)}, u32[]{:S(2)}) %collective-permute-start.34) | collective-permute-done | bytes 32800 | tf_op jit(solution)/shard_map/ppermute | solution.py:201
  79.7 0.6 shard_map.137
  (48 shorter events, 1.9 us)
Async XLA Ops:
  0.0 10.7 %copy-start.2 = (bf16[128,2048]{1,0:T(8,128)(2,1)S(1)}, bf16[128,2048]{1,0:T(8,128)(2,1)}, u32[]{:S(2)}) copy-start(bf16[128,2048]{1,0:T(8,128)(2,1)} %refs_6_.1) | copy-start | bytes 1572868
  3.8 6.9 %collective-permute-start.3 = (bf16[256,2048]{1,0:T(8,128)(2,1)S(1)}, bf16[256,2048]{1,0:T(8,128)(2,1)S(1)}, u32[]{:S(2)}, u32[]{:S(2)}) collective-permute-start(bf16[256,2048]{1,0:T(8,128)(2,1)S(1)} %get-tuple-element.45.refs_4_), channel_id=1, source_target_pairs={{0,2},{1,3},{2,0},{3,1},{4,6},{5,7},{6,4},{7,5},{8,10},{9,11},{10,... | collective-permute-start | bytes 3145736 | tf_op jit(solution)/shard_map/ppermute | solution.py:201
  4.3 2.7 %copy-start.5 = (f32[128,8]{0,1:T(8,128)S(1)}, f32[128,8]{0,1:T(8,128)}, u32[]{:S(2)}) copy-start(f32[128,8]{0,1:T(8,128)} %param.21) | copy-start | bytes 12292
  4.3 2.7 %copy-start.4 = (s32[128,8]{0,1:T(8,128)S(1)}, s32[128,8]{0,1:T(8,128)}, u32[]{:S(2)}) copy-start(s32[128,8]{0,1:T(8,128)} %param.20) | copy-start | bytes 12292
  4.3 4.0 %collective-permute-start = (bf16[32,256]{1,0:T(8,128)(2,1)S(1)}, bf16[32,256]{1,0:T(8,128)(2,1)S(1)}, u32[]{:S(2)}, u32[]{:S(2)}) collective-permute-start(bf16[32,256]{1,0:T(8,128)(2,1)S(1)} %get-tuple-element.37), channel_id=1, source_target_pairs={{0,3},{1,2},{2,1},{3,0},{4,7},{5,6},{6,5},{7,4},{8,11},{9,10},{10,... | collective-permute-start | bytes 49160 | tf_op jit(solution)/shard_map/ppermute | solution.py:201
  6.9 3.7 %collective-permute-start.1 = (bf16[32,256]{1,0:T(8,128)(2,1)S(1)}, bf16[32,256]{1,0:T(8,128)(2,1)S(1)}, u32[]{:S(2)}, u32[]{:S(2)}) collective-permute-start(bf16[32,256]{1,0:T(8,128)(2,1)S(1)} %get-tuple-element.42), channel_id=1, source_target_pairs={{0,1},{1,0},{2,3},{3,2},{4,5},{5,4},{6,7},{7,6},{8,9},{9,8},{10,11... | collective-permute-start | bytes 49160 | tf_op jit(solution)/shard_map/ppermute | solution.py:201
  7.0 3.7 %collective-permute-start.2 = (bf16[32,256]{1,0:T(8,128)(2,1)S(1)}, bf16[32,256]{1,0:T(8,128)(2,1)S(1)}, u32[]{:S(2)}, u32[]{:S(2)}) collective-permute-start(bf16[32,256]{1,0:T(8,128)(2,1)S(1)} %get-tuple-element.43), channel_id=1, source_target_pairs={{0,2},{1,3},{2,0},{3,1},{4,6},{5,7},{6,4},{7,5},{8,10},{9,11},{10,... | collective-permute-start | bytes 49160 | tf_op jit(solution)/shard_map/ppermute | solution.py:201
  7.1 0.7 copy-start.6
  10.7 1.1 %copy-start = (bf16[1,2048,192]{1,2,0:T(8,128)(2,1)S(1)}, bf16[1,2048,192]{1,2,0:T(8,128)(2,1)}, u32[]{:S(2)}) copy-start(bf16[1,2048,192]{1,2,0:T(8,128)(2,1)} %param.23) | copy-start | bytes 2359300
  10.7 1.4 %copy-start.1 = (bf16[1,2048,192]{1,2,0:T(8,128)(2,1)S(1)}, bf16[1,2048,192]{1,2,0:T(8,128)(2,1)}, u32[]{:S(2)}) copy-start(bf16[1,2048,192]{1,2,0:T(8,128)(2,1)} %param.24) | copy-start | bytes 2359300
  11.8 8.1 %copy-start.3 = (f32[2048]{0:T(1024)S(1)}, f32[2048]{0:T(1024)}, u32[]{:S(2)}) copy-start(f32[2048]{0:T(1024)} %param.19) | copy-start | bytes 24580
  11.8 39.6 %collective-permute-start.4 = (bf16[192,2048]{1,0:T(8,128)(2,1)S(1)}, bf16[192,2048]{1,0:T(8,128)(2,1)S(1)}, u32[]{:S(2)}, u32[]{:S(2)}) collective-permute-start(bf16[192,2048]{1,0:T(8,128)(2,1)S(1)} %bitcast.9), channel_id=1, source_target_pairs={{0,2},{1,3},{2,0},{3,1},{4,6},{5,7},{6,4},{7,5},{8,10},{9,11},{10,... | collective-permute-start | bytes 2359304 | tf_op jit(solution)/shard_map/ppermute | solution.py:201
  12.1 39.9 %collective-permute-start.5 = (bf16[192,2048]{1,0:T(8,128)(2,1)S(1)}, bf16[192,2048]{1,0:T(8,128)(2,1)S(1)}, u32[]{:S(2)}, u32[]{:S(2)}) collective-permute-start(bf16[192,2048]{1,0:T(8,128)(2,1)S(1)} %bitcast.12), channel_id=1, source_target_pairs={{0,2},{1,3},{2,0},{3,1},{4,6},{5,7},{6,4},{7,5},{8,10},{9,11},{10,... | collective-permute-start | bytes 2359304 | tf_op jit(solution)/shard_map/ppermute | solution.py:201
  12.3 4.5 %collective-permute-start.6 = (bf16[64,512]{1,0:T(8,128)(2,1)S(1)}, bf16[64,512]{1,0:T(8,128)(2,1)S(1)}, u32[]{:S(2)}, u32[]{:S(2)}) collective-permute-start(bf16[64,512]{1,0:T(8,128)(2,1)S(1)} %get-tuple-element.46), channel_id=1, source_target_pairs={{0,1},{1,0},{2,3},{3,2},{4,5},{5,4},{6,7},{7,6},{8,9},{9,8},{10,11... | collective-permute-start | bytes 196616 | tf_op jit(solution)/shard_map/ppermute | solution.py:201
  12.5 5.1 %collective-permute-start.7 = (bf16[64,512]{1,0:T(8,128)(2,1)S(1)}, bf16[64,512]{1,0:T(8,128)(2,1)S(1)}, u32[]{:S(2)}, u32[]{:S(2)}) collective-permute-start(bf16[64,512]{1,0:T(8,128)(2,1)S(1)} %get-tuple-element.50), channel_id=1, source_target_pairs={{0,4},{1,5},{2,6},{3,7},{4,0},{5,1},{6,2},{7,3},{8,12},{9,13},{10,... | collective-permute-start | bytes 196616 | tf_op jit(solution)/shard_map/ppermute | solution.py:201
  14.4 5.5 %collective-permute-start.8 = (bf16[64,512]{1,0:T(8,128)(2,1)S(1)}, bf16[64,512]{1,0:T(8,128)(2,1)S(1)}, u32[]{:S(2)}, u32[]{:S(2)}) collective-permute-start(bf16[64,512]{1,0:T(8,128)(2,1)S(1)} %get-tuple-element.51), channel_id=1, source_target_pairs={{0,5},{1,4},{2,7},{3,6},{4,1},{5,0},{6,3},{7,2},{8,13},{9,12},{10,... | collective-permute-start | bytes 196616 | tf_op jit(solution)/shard_map/ppermute | solution.py:201
  16.8 19.3 %collective-permute-start.16 = (bf16[192,512]{1,0:T(8,128)(2,1)S(1)}, bf16[192,512]{1,0:T(8,128)(2,1)S(1)}, u32[]{:S(2)}, u32[]{:S(2)}) collective-permute-start(bf16[192,512]{1,0:T(8,128)(2,1)S(1)} %get-tuple-element.59), channel_id=1, source_target_pairs={{0,1},{1,0},{2,3},{3,2},{4,5},{5,4},{6,7},{7,6},{8,9},{9,8},{10,11... | collective-permute-start | bytes 589832 | tf_op jit(solution)/shard_map/ppermute | solution.py:201
  20.1 4.5 %collective-permute-start.9 = (bf16[72,512]{1,0:T(8,128)(2,1)S(1)}, bf16[72,512]{1,0:T(8,128)(2,1)S(1)}, u32[]{:S(2)}, u32[]{:S(2)}) collective-permute-start(bf16[72,512]{1,0:T(8,128)(2,1)S(1)} %get-tuple-element.53.refs_0_.refs_6_), channel_id=1, source_target_pairs={{0,8},{1,9},{2,10},{3,11},{4,12},{5,13},{6,14},{7,15},{8,0},{9,1},... | collective-permute-start | bytes 221192 | tf_op jit(solution)/shard_map/ppermute | solution.py:201
  21.7 6.3 %collective-permute-start.24 = (bf16[72,512]{1,0:T(8,128)(2,1)S(1)}, bf16[72,512]{1,0:T(8,128)(2,1)S(1)}, u32[]{:S(2)}, u32[]{:S(2)}) collective-permute-start(bf16[72,512]{1,0:T(8,128)(2,1)S(1)} %get-tuple-element.53.refs_0_.refs_6_), channel_id=1, source_target_pairs={{0,16},{1,17},{2,18},{3,19},{4,20},{5,21},{6,22},{7,23},{8,24},{9,... | collective-permute-start | bytes 221192 | tf_op jit(solution)/shard_map/ppermute | solution.py:201
  24.7 11.5 %collective-permute-start.17 = (bf16[192,512]{1,0:T(8,128)(2,1)S(1)}, bf16[192,512]{1,0:T(8,128)(2,1)S(1)}, u32[]{:S(2)}, u32[]{:S(2)}) collective-permute-start(bf16[192,512]{1,0:T(8,128)(2,1)S(1)} %get-tuple-element.60), channel_id=1, source_target_pairs={{0,4},{1,5},{2,6},{3,7},{4,0},{5,1},{6,2},{7,3},{8,12},{9,13},{10,... | collective-permute-start | bytes 589832 | tf_op jit(solution)/shard_map/ppermute | solution.py:201
  28.0 6.2 %collective-permute-start.25 = (bf16[72,512]{1,0:T(8,128)(2,1)S(1)}, bf16[72,512]{1,0:T(8,128)(2,1)S(1)}, u32[]{:S(2)}, u32[]{:S(2)}) collective-permute-start(bf16[72,512]{1,0:T(8,128)(2,1)S(1)} %get-tuple-element.53.refs_0_.refs_6_), channel_id=1, source_target_pairs={{0,24},{1,25},{2,26},{3,27},{4,28},{5,29},{6,30},{7,31},{8,16},{9,... | collective-permute-start | bytes 221192 | tf_op jit(solution)/shard_map/ppermute | solution.py:201
  34.2 7.3 %collective-permute-start.18 = (bf16[192,512]{1,0:T(8,128)(2,1)S(1)}, bf16[192,512]{1,0:T(8,128)(2,1)S(1)}, u32[]{:S(2)}, u32[]{:S(2)}) collective-permute-start(bf16[192,512]{1,0:T(8,128)(2,1)S(1)} %get-tuple-element.61), channel_id=1, source_target_pairs={{0,5},{1,4},{2,7},{3,6},{4,1},{5,0},{6,3},{7,2},{8,13},{9,12},{10,... | collective-permute-start | bytes 589832 | tf_op jit(solution)/shard_map/ppermute | solution.py:201
  36.1 6.9 %collective-permute-start.19 = (bf16[192,512]{1,0:T(8,128)(2,1)S(1)}, bf16[192,512]{1,0:T(8,128)(2,1)S(1)}, u32[]{:S(2)}, u32[]{:S(2)}) collective-permute-start(bf16[192,512]{1,0:T(8,128)(2,1)S(1)} %get-tuple-element.58.refs_4_), channel_id=1, source_target_pairs={{0,2},{1,3},{2,0},{3,1},{4,6},{5,7},{6,4},{7,5},{8,10},{9,11},{10,... | collective-permute-start | bytes 589832 | tf_op jit(solution)/shard_map/ppermute | solution.py:201
  36.1 10.3 %collective-permute-start.10 = (bf16[128,512]{1,0:T(8,128)(2,1)S(1)}, bf16[128,512]{1,0:T(8,128)(2,1)S(1)}, u32[]{:S(2)}, u32[]{:S(2)}) collective-permute-start(bf16[128,512]{1,0:T(8,128)(2,1)S(1)} %shard_map.130.refs_8_), channel_id=1, source_target_pairs={{0,1},{1,0},{2,3},{3,2},{4,5},{5,4},{6,7},{7,6},{8,9},{9,8},{10,11... | collective-permute-start | bytes 393224 | tf_op jit(solution)/shard_map/ppermute | solution.py:201
  41.4 5.3 %collective-permute-start.11 = (bf16[128,512]{1,0:T(8,128)(2,1)S(1)}, bf16[128,512]{1,0:T(8,128)(2,1)S(1)}, u32[]{:S(2)}, u32[]{:S(2)}) collective-permute-start(bf16[128,512]{1,0:T(8,128)(2,1)S(1)} %shard_map.130.refs_8_), channel_id=1, source_target_pairs={{0,4},{1,5},{2,6},{3,7},{4,0},{5,1},{6,2},{7,3},{8,12},{9,13},{10,... | collective-permute-start | bytes 393224 | tf_op jit(solution)/shard_map/ppermute | solution.py:201
  43.0 6.4 %collective-permute-start.12 = (bf16[128,512]{1,0:T(8,128)(2,1)S(1)}, bf16[128,512]{1,0:T(8,128)(2,1)S(1)}, u32[]{:S(2)}, u32[]{:S(2)}) collective-permute-start(bf16[128,512]{1,0:T(8,128)(2,1)S(1)} %shard_map.130.refs_8_), channel_id=1, source_target_pairs={{0,5},{1,4},{2,7},{3,6},{4,1},{5,0},{6,3},{7,2},{8,13},{9,12},{10,... | collective-permute-start | bytes 393224 | tf_op jit(solution)/shard_map/ppermute | solution.py:201
  46.4 5.0 %collective-permute-start.26 = (bf16[128,512]{1,0:T(8,128)(2,1)S(1)}, bf16[128,512]{1,0:T(8,128)(2,1)S(1)}, u32[]{:S(2)}, u32[]{:S(2)}) collective-permute-start(bf16[128,512]{1,0:T(8,128)(2,1)S(1)} %shard_map.133.refs_8_), channel_id=1, source_target_pairs={{0,1},{1,0},{2,3},{3,2},{4,5},{5,4},{6,7},{7,6},{8,9},{9,8},{10,11... | collective-permute-start | bytes 393224 | tf_op jit(solution)/shard_map/ppermute | solution.py:201
  46.7 13.3 %collective-permute-start.20 = (bf16[192,512]{1,0:T(8,128)(2,1)S(1)}, bf16[192,512]{1,0:T(8,128)(2,1)S(1)}, u32[]{:S(2)}, u32[]{:S(2)}) collective-permute-start(bf16[192,512]{1,0:T(8,128)(2,1)S(1)} %collective-permute-done.16.refs_5_), channel_id=1, source_target_pairs={{0,2},{1,3},{2,0},{3,1},{4,6},{5,7},{6,4},{7,5},{8,10},{9,11},{10,... | collective-permute-start | bytes 589832 | tf_op jit(solution)/shard_map/ppermute | solution.py:201
  49.3 5.3 %collective-permute-start.27 = (bf16[128,512]{1,0:T(8,128)(2,1)S(1)}, bf16[128,512]{1,0:T(8,128)(2,1)S(1)}, u32[]{:S(2)}, u32[]{:S(2)}) collective-permute-start(bf16[128,512]{1,0:T(8,128)(2,1)S(1)} %shard_map.133.refs_8_), channel_id=1, source_target_pairs={{0,4},{1,5},{2,6},{3,7},{4,0},{5,1},{6,2},{7,3},{8,12},{9,13},{10,... | collective-permute-start | bytes 393224 | tf_op jit(solution)/shard_map/ppermute | solution.py:201
  51.4 12.0 %collective-permute-start.21 = (bf16[192,512]{1,0:T(8,128)(2,1)S(1)}, bf16[192,512]{1,0:T(8,128)(2,1)S(1)}, u32[]{:S(2)}, u32[]{:S(2)}) collective-permute-start(bf16[192,512]{1,0:T(8,128)(2,1)S(1)} %collective-permute-done.17.refs_6_), channel_id=1, source_target_pairs={{0,2},{1,3},{2,0},{3,1},{4,6},{5,7},{6,4},{7,5},{8,10},{9,11},{10,... | collective-permute-start | bytes 589832 | tf_op jit(solution)/shard_map/ppermute | solution.py:201
  51.5 12.1 %collective-permute-start.22 = (bf16[192,512]{1,0:T(8,128)(2,1)S(1)}, bf16[192,512]{1,0:T(8,128)(2,1)S(1)}, u32[]{:S(2)}, u32[]{:S(2)}) collective-permute-start(bf16[192,512]{1,0:T(8,128)(2,1)S(1)} %collective-permute-done.18.refs_7_), channel_id=1, source_target_pairs={{0,2},{1,3},{2,0},{3,1},{4,6},{5,7},{6,4},{7,5},{8,10},{9,11},{10,... | collective-permute-start | bytes 589832 | tf_op jit(solution)/shard_map/ppermute | solution.py:201
  52.0 6.6 %collective-permute-start.28 = (bf16[128,512]{1,0:T(8,128)(2,1)S(1)}, bf16[128,512]{1,0:T(8,128)(2,1)S(1)}, u32[]{:S(2)}, u32[]{:S(2)}) collective-permute-start(bf16[128,512]{1,0:T(8,128)(2,1)S(1)} %shard_map.133.refs_8_), channel_id=1, source_target_pairs={{0,5},{1,4},{2,7},{3,6},{4,1},{5,0},{6,3},{7,2},{8,13},{9,12},{10,... | collective-permute-start | bytes 393224 | tf_op jit(solution)/shard_map/ppermute | solution.py:201
  54.7 10.3 %collective-permute-start.13 = (bf16[128,384]{1,0:T(8,128)(2,1)S(1)}, bf16[128,384]{1,0:T(8,128)(2,1)S(1)}, u32[]{:S(2)}, u32[]{:S(2)}) collective-permute-start(bf16[128,384]{1,0:T(8,128)(2,1)S(1)} %shard_map.131.refs_0_), channel_id=1, source_target_pairs={{0,1},{1,0},{2,3},{3,2},{4,5},{5,4},{6,7},{7,6},{8,9},{9,8},{10,11... | collective-permute-start | bytes 294920 | tf_op jit(solution)/shard_map/ppermute | solution.py:201
  58.6 8.5 %collective-permute-start.14 = (bf16[128,384]{1,0:T(8,128)(2,1)S(1)}, bf16[128,384]{1,0:T(8,128)(2,1)S(1)}, u32[]{:S(2)}, u32[]{:S(2)}) collective-permute-start(bf16[128,384]{1,0:T(8,128)(2,1)S(1)} %shard_map.131.refs_0_), channel_id=1, source_target_pairs={{0,4},{1,5},{2,6},{3,7},{4,0},{5,1},{6,2},{7,3},{8,12},{9,13},{10,... | collective-permute-start | bytes 294920 | tf_op jit(solution)/shard_map/ppermute | solution.py:201
  60.0 7.0 %collective-permute-start.15 = (bf16[128,384]{1,0:T(8,128)(2,1)S(1)}, bf16[128,384]{1,0:T(8,128)(2,1)S(1)}, u32[]{:S(2)}, u32[]{:S(2)}) collective-permute-start(bf16[128,384]{1,0:T(8,128)(2,1)S(1)} %shard_map.131.refs_0_), channel_id=1, source_target_pairs={{0,5},{1,4},{2,7},{3,6},{4,1},{5,0},{6,3},{7,2},{8,13},{9,12},{10,... | collective-permute-start | bytes 294920 | tf_op jit(solution)/shard_map/ppermute | solution.py:201
  63.5 4.7 %collective-permute-start.29 = (bf16[128,384]{1,0:T(8,128)(2,1)S(1)}, bf16[128,384]{1,0:T(8,128)(2,1)S(1)}, u32[]{:S(2)}, u32[]{:S(2)}) collective-permute-start(bf16[128,384]{1,0:T(8,128)(2,1)S(1)} %shard_map.134.refs_0_), channel_id=1, source_target_pairs={{0,1},{1,0},{2,3},{3,2},{4,5},{5,4},{6,7},{7,6},{8,9},{9,8},{10,11... | collective-permute-start | bytes 294920 | tf_op jit(solution)/shard_map/ppermute | solution.py:201
  63.6 4.9 %collective-permute-start.30 = (bf16[128,384]{1,0:T(8,128)(2,1)S(1)}, bf16[128,384]{1,0:T(8,128)(2,1)S(1)}, u32[]{:S(2)}, u32[]{:S(2)}) collective-permute-start(bf16[128,384]{1,0:T(8,128)(2,1)S(1)} %shard_map.134.refs_0_), channel_id=1, source_target_pairs={{0,4},{1,5},{2,6},{3,7},{4,0},{5,1},{6,2},{7,3},{8,12},{9,13},{10,... | collective-permute-start | bytes 294920 | tf_op jit(solution)/shard_map/ppermute | solution.py:201
  65.0 5.5 %collective-permute-start.31 = (bf16[128,384]{1,0:T(8,128)(2,1)S(1)}, bf16[128,384]{1,0:T(8,128)(2,1)S(1)}, u32[]{:S(2)}, u32[]{:S(2)}) collective-permute-start(bf16[128,384]{1,0:T(8,128)(2,1)S(1)} %shard_map.134.refs_0_), channel_id=1, source_target_pairs={{0,5},{1,4},{2,7},{3,6},{4,1},{5,0},{6,3},{7,2},{8,13},{9,12},{10,... | collective-permute-start | bytes 294920 | tf_op jit(solution)/shard_map/ppermute | solution.py:201
  67.5 5.4 %collective-permute-start.23 = (bf16[64,512]{1,0:T(8,128)(2,1)S(1)}, bf16[64,512]{1,0:T(8,128)(2,1)S(1)}, u32[]{:S(2)}, u32[]{:S(2)}) collective-permute-start(bf16[64,512]{1,0:T(8,128)(2,1)S(1)} %get-tuple-element.64), channel_id=1, source_target_pairs={{0,8},{1,9},{2,10},{3,11},{4,12},{5,13},{6,14},{7,15},{8,0},{9,1},... | collective-permute-start | bytes 196616 | tf_op jit(solution)/shard_map/ppermute | solution.py:201
  71.0 5.2 %collective-permute-start.32 = (bf16[64,512]{1,0:T(8,128)(2,1)S(1)}, bf16[64,512]{1,0:T(8,128)(2,1)S(1)}, u32[]{:S(2)}, u32[]{:S(2)}) collective-permute-start(bf16[64,512]{1,0:T(8,128)(2,1)S(1)} %get-tuple-element.65), channel_id=1, source_target_pairs={{0,16},{1,17},{2,18},{3,19},{4,20},{5,21},{6,22},{7,23},{8,24},{9,... | collective-permute-start | bytes 196616 | tf_op jit(solution)/shard_map/ppermute | solution.py:201
  72.4 6.1 %collective-permute-start.33 = (bf16[64,512]{1,0:T(8,128)(2,1)S(1)}, bf16[64,512]{1,0:T(8,128)(2,1)S(1)}, u32[]{:S(2)}, u32[]{:S(2)}) collective-permute-start(bf16[64,512]{1,0:T(8,128)(2,1)S(1)} %get-tuple-element.66), channel_id=1, source_target_pairs={{0,24},{1,25},{2,26},{3,27},{4,28},{5,29},{6,30},{7,31},{8,16},{9,... | collective-permute-start | bytes 196616 | tf_op jit(solution)/shard_map/ppermute | solution.py:201
  78.5 1.3 %collective-permute-start.34 = (bf16[64,256]{1,0:T(8,128)(2,1)S(1)}, bf16[64,256]{1,0:T(8,128)(2,1)S(1)}, u32[]{:S(2)}, u32[]{:S(2)}) collective-permute-start(bf16[64,256]{1,0:T(8,128)(2,1)S(1)} %get-tuple-element.68), channel_id=1, source_target_pairs={{0,2},{1,3},{2,0},{3,1},{4,6},{5,7},{6,4},{7,5},{8,10},{9,11},{10,... | collective-permute-start | bytes 98312 | tf_op jit(solution)/shard_map/ppermute | solution.py:201
where the time goes:
time: 80.5 us; the launch traced here: 80.4 us
  starting transfers between devices  34.8 us (43%)
  waiting for transfers between devices  34.4 us (43%)
  Pallas kernels  9.5 us (12%)
  local copies, waits for them, and re-layouts  1.49 us (2%)
    ppermute x35, starting transfers between devices, moved(): return lax.ppermute(value, AXES, pairs)  34.8 us
    ppermute x35, waiting for transfers between devices, moved(): return lax.ppermute(value, AXES, pairs)  34.4 us
    pallas_call x11, Pallas kernels, called(): pl.pallas_call(kernel, out_shape=tuple(outs), in_specs=[in_smem()] * n_sm...  5.74 us
    pallas_call x1, Pallas kernels, attention(): pl.pallas_call(lambda *refs: attention_kernel(chips, *refs), out_shape=tu...  3.77 us
  transfers between devices with their start and end apart: 35, of which 17 were waited for; matrix products, arithmetic and copies ran while one was open for 0% of the time, Pallas kernels for 6%

commit v1 on v0

--- a/solution.py
+++ b/solution.py
@@ -176,6 +176,7 @@
 BF16 = jnp.bfloat16
 AXES = ("req", "kvh", "exp")
 STEP = 16
+BATCH = 2
 VMEM_LIMIT = 16 * 2**20
 
 
@@ -242,15 +243,14 @@
 
 
 def attention_kernel(chips, lengths, query, key, value, weight, down, *refs):
-    blocks, weight_copy, pieces = refs[:4], refs[4], refs[5:-5]
-    limits, rows_ref, key_ref, value_ref, sems = refs[-5:]
+    blocks, weight_copy, pieces = refs[:4], refs[4], refs[5:-7]
+    limits, rows_ref, wide_ref, done_ref, key_ref, value_ref, sems = refs[-7:]
     _, _, core, side = place()
     n_rows = query.shape[0]
     span, head_dim = key.shape[2], key.shape[3]
     heads = query.shape[1] // head_dim
     n = STEP
     steps = n_rows // n
-    half = steps // 2
 
     def cached(step, index):
         source, target = ((key, key_ref), (value, value_ref))[index]
@@ -283,50 +283,51 @@
     same = request == owner
     for copy in begin:
         copy.wait()
-
-    @pl.loop(0, steps)
-    def _(step):
-        here = pl.ds(pl.multiple_of(step * n, n), n)
-        rows = jnp.concatenate(
-            [rows_ref[here, head * head_dim : (head + 1) * head_dim] for head in range(heads)],
-            axis=0,
-        )
-        limit = jnp.zeros((1, n * span), jnp.int32)
-        first = side * n_rows + step * n
-        for index in range(n):
-            limit = jnp.where(owner == index, limits[first + index], limit)
-        valid = same & (position < limit)
-        cached(step, 0).wait()
-        scores = nt_dot(rows, key_ref[here].reshape(n * span, head_dim)) * head_dim ** (-0.5)
-        scores = jnp.where(valid, scores, -1e30)
+    wide_ref[...] = rows_ref[...].astype(F32)
+
+    for batch in range(0, steps, BATCH):
+        batch_steps = range(batch, batch + BATCH)
+        masked = []
+        for step in batch_steps:
+            here = slice(step * n, (step + 1) * n)
+            rows = jnp.concatenate(
+                [wide_ref[here, head * head_dim : (head + 1) * head_dim] for head in range(heads)],
+                axis=0,
+            ).astype(BF16)
+            limit = jnp.zeros((1, n * span), jnp.int32)
+            first = side * n_rows + step * n
+            for index in range(n):
+                limit = jnp.where(owner == index, limits[first + index], limit)
+            valid = same & (position < limit)
+            if step == batch:
+                for ahead in batch_steps:
+                    cached(ahead, 0).wait()
+                    cached(ahead, 1).wait()
+            scores = nt_dot(rows, key_ref[here].reshape(n * span, head_dim)) * head_dim ** (-0.5)
+            masked.append(jnp.where(valid, scores, -1e30))
+        scores = jnp.concatenate(masked, axis=0)
         peak = jnp.max(scores, axis=1, keepdims=True)
         weights = jnp.exp(scores - peak)
         total = jnp.sum(weights, axis=1, keepdims=True)
         high = weights.astype(BF16)
         low = (weights - high.astype(F32)).astype(BF16)
-        cached(step, 1).wait()
-        held = value_ref[here].reshape(n * span, head_dim)
-        both = nn_dot(jnp.concatenate([high, low], axis=0), held)
-        numer = (both[: heads * n] + both[heads * n :]) / total
-        by_head = [numer[head * n : (head + 1) * n].astype(BF16) for head in range(heads)]
-        lower = jnp.concatenate(by_head[: heads // 2], axis=1)
-        upper = jnp.concatenate(by_head[heads // 2 :], axis=1)
-        near = jnp.where(side == 0, lower, upper)
-        far = jnp.where(side == 0, upper, lower)
-        passed = step >= half
-        spot = pl.ds(pl.multiple_of((step - jnp.where(passed, half, 0)) * n, n), n)
-        at_home = passed == (core == 1)
-
-        @pl.when(at_home)
-        def _():
-            blocks[0][spot, :] = near
-            blocks[1][spot, :] = far
-
-        @pl.when(jnp.logical_not(at_home))
-        def _():
-            blocks[2][spot, :] = near
-            blocks[3][spot, :] = far
-
+        for step in batch_steps:
+            here = slice(step * n, (step + 1) * n)
+            own = slice((step - batch) * heads * n, (step - batch + 1) * heads * n)
+            held = value_ref[here].reshape(n * span, head_dim)
+            both = nn_dot(jnp.concatenate([high[own], low[own]], axis=0), held)
+            numer = (both[: heads * n] + both[heads * n :]) / total[own]
+            for head in range(heads):
+                done_ref[here, head * head_dim : (head + 1) * head_dim] = numer[
+                    head * n : (head + 1) * n
+                ]
+
+    half, width = n_rows // 2, query.shape[1] // 2
+    for index, out in enumerate(blocks):
+        at = core if index < 2 else 1 - core
+        towards = side if index % 2 == 0 else 1 - side
+        spot = pl.ds(pl.multiple_of(at * half, half), half)
+        out[...] = done_ref[spot, pl.ds(pl.multiple_of(towards * width, width), width)].astype(BF16)
     for copy in rest:
         copy.wait()
 
@@ -346,6 +347,8 @@
         scratch_shapes=[
             pltpu.SMEM(lengths.shape, jnp.int32),
             pltpu.VMEM(queries.shape, BF16),
+            pltpu.VMEM(queries.shape, F32),
+            pltpu.VMEM(queries.shape, F32),
             pltpu.VMEM(keys.shape, BF16),
             pltpu.VMEM(values.shape, BF16),
             pltpu.SemaphoreType.DMA((3 + 2 * (rows // STEP) + 2 * len(chips),)),
@@ -468,8 +471,9 @@
             part = part_ref[:, index * block : (index + 1) * block]
             weight = jnp.concatenate([ref[:, where] for ref in weights], axis=0)
             product = nt_dot(part, weight)
-            plain = part.astype(F32) / gain[:, where]
-            square = jnp.sum(plain * plain, axis=1, keepdims=True)
+            plain = part.astype(F32)
+            scale = gain[:, where]
+            square = jnp.sum(plain * plain * (1.0 / (scale * scale)), axis=1, keepdims=True)
             gates = product if gates is None else gates + product
             squares = square if squares is None else squares + square
     scale = lax.rsqrt(squares / d_model + 1e-06)

time: 80.5 us -> 79.4 us (0.986)
  Pallas kernels: 9.5 us -> 8.41 us
    pallas_call x1, Pallas kernels: 3.77 us -> 2.67 us  [attention(): pl.pallas_call(lambda *refs: attention_kernel(chips, *refs), out_shape=tu...]
where the time goes in v1:
time: 79.4 us; the launch traced here: 79.3 us
  starting transfers between devices  34.8 us (44%)
  waiting for transfers between devices  34.4 us (43%)
  Pallas kernels  8.41 us (11%)
  local copies, waits for them, and re-layouts  1.49 us (2%)
    ppermute x35, starting transfers between devices, moved(): return lax.ppermute(value, AXES, pairs)  34.8 us
    ppermute x35, waiting for transfers between devices, moved(): return lax.ppermute(value, AXES, pairs)  34.4 us
    pallas_call x11, Pallas kernels, called(): pl.pallas_call(kernel, out_shape=tuple(outs), in_specs=[in_smem()] * n_sm...  5.74 us
    pallas_call x1, Pallas kernels, attention(): pl.pallas_call(lambda *refs: attention_kernel(chips, *refs), out_shape=tu...  2.67 us
  transfers between devices with their start and end apart: 35, of which 17 were waited for; matrix products, arithmetic and copies ran while one was open for 0% of the time, Pallas kernels for 6%

profile of v1, /device:TPU:0, one launch (start us, length us, event | category | flops | bytes accessed | tf_op | source)
XLA Modules:
  0.0 79.3 jit_solution(9207226558481317562)
XLA Ops:
  0.0 2.7 %attention.1 = (bf16[32,256]{1,0:T(8,128)(2,1)S(1)}, bf16[32,256]{1,0:T(8,128)(2,1)S(1)}, bf16[32,256]{1,0:T(8,128)(2,1)S(1)}, bf16[32,256]{1,0:T(8,128)(2,1)S(1...) custom-call(s32[128]{0:T(128)} %refs_0_.1, ...), custom_call_target="tpu_custom_call" | custom-call | flops 201326592 | bytes 2097152 | tf_op jit(solution)/shard_map/attention/pallas_call | solution.py:342
  2.7 0.6 collective-permute-start.3
  3.2 2.6 %collective-permute-start = (bf16[32,256]{1,0:T(8,128)(2,1)S(1)}, bf16[32,256]{1,0:T(8,128)(2,1)S(1)}, u32[]{:S(2)}, u32[]{:S(2)}) collective-permute-start(bf16[32,256]{1,0:T(8,128)(2,1)S(1)} %get-tuple-element.37), channel_id=1, source_target_pairs={{0,3},{1,2},{2,1},{3,0},{4,7},{5,6},{6,5},{7,4},{8,11},{9,10},{10,... | collective-permute-start | bytes 49160 | tf_op jit(solution)/shard_map/ppermute | solution.py:202
  6.0 0.6 copy-done.6
  6.6 0.6 shard_map.127
  7.3 2.3 %collective-permute-done.1.refs_1_ = bf16[32,256]{1,0:T(8,128)(2,1)S(1)} collective-permute-done((bf16[32,256]{1,0:T(8,128)(2,1)S(1)}, bf16[32,256]{1,0:T(8,128)(2,1)S(1)}, u32[]{:S(2)}, u32[]{:S(2)}) %collective-permute-start.1) | collective-permute-done | bytes 16416 | tf_op jit(solution)/shard_map/ppermute | solution.py:202
  9.6 0.5 shard_map.128
  10.1 0.6 copy-done
  11.4 1.9 %collective-permute-start.7 = (bf16[64,512]{1,0:T(8,128)(2,1)S(1)}, bf16[64,512]{1,0:T(8,128)(2,1)S(1)}, u32[]{:S(2)}, u32[]{:S(2)}) collective-permute-start(bf16[64,512]{1,0:T(8,128)(2,1)S(1)} %get-tuple-element.50), channel_id=1, source_target_pairs={{0,4},{1,5},{2,6},{3,7},{4,0},{5,1},{6,2},{7,3},{8,12},{9,13},{10,... | collective-permute-start | bytes 196616 | tf_op jit(solution)/shard_map/ppermute | solution.py:202
  13.3 1.4 %collective-permute-start.8 = (bf16[64,512]{1,0:T(8,128)(2,1)S(1)}, bf16[64,512]{1,0:T(8,128)(2,1)S(1)}, u32[]{:S(2)}, u32[]{:S(2)}) collective-permute-start(bf16[64,512]{1,0:T(8,128)(2,1)S(1)} %get-tuple-element.51), channel_id=1, source_target_pairs={{0,5},{1,4},{2,7},{3,6},{4,1},{5,0},{6,3},{7,2},{8,13},{9,12},{10,... | collective-permute-start | bytes 196616 | tf_op jit(solution)/shard_map/ppermute | solution.py:202
  14.7 1.0 %collective-permute-done.6.refs_1_ = bf16[64,512]{1,0:T(8,128)(2,1)S(1)} collective-permute-done((bf16[64,512]{1,0:T(8,128)(2,1)S(1)}, bf16[64,512]{1,0:T(8,128)(2,1)S(1)}, u32[]{:S(2)}, u32[]{:S(2)}) %collective-permute-start.6) | collective-permute-done | bytes 65568 | tf_op jit(solution)/shard_map/ppermute | solution.py:202
  15.8 0.7 collective-permute-done.7.refs_2_
  16.5 2.3 %collective-permute-done.8.refs_3_ = bf16[64,512]{1,0:T(8,128)(2,1)S(1)} collective-permute-done((bf16[64,512]{1,0:T(8,128)(2,1)S(1)}, bf16[64,512]{1,0:T(8,128)(2,1)S(1)}, u32[]{:S(2)}, u32[]{:S(2)}) %collective-permute-start.8) | collective-permute-done | bytes 65568 | tf_op jit(solution)/shard_map/ppermute | solution.py:202
  19.0 1.6 %collective-permute-start.9 = (bf16[72,512]{1,0:T(8,128)(2,1)S(1)}, bf16[72,512]{1,0:T(8,128)(2,1)S(1)}, u32[]{:S(2)}, u32[]{:S(2)}) collective-permute-start(bf16[72,512]{1,0:T(8,128)(2,1)S(1)} %get-tuple-element.53.refs_0_.refs_6_), channel_id=1, source_target_pairs={{0,8},{1,9},{2,10},{3,11},{4,12},{5,13},{6,14},{7,15},{8,0},{9,1},... | collective-permute-start | bytes 221192 | tf_op jit(solution)/shard_map/ppermute | solution.py:202
  20.6 2.6 %collective-permute-start.24 = (bf16[72,512]{1,0:T(8,128)(2,1)S(1)}, bf16[72,512]{1,0:T(8,128)(2,1)S(1)}, u32[]{:S(2)}, u32[]{:S(2)}) collective-permute-start(bf16[72,512]{1,0:T(8,128)(2,1)S(1)} %get-tuple-element.53.refs_0_.refs_6_), channel_id=1, source_target_pairs={{0,16},{1,17},{2,18},{3,19},{4,20},{5,21},{6,22},{7,23},{8,24},{9,... | collective-permute-start | bytes 221192 | tf_op jit(solution)/shard_map/ppermute | solution.py:202
  23.2 0.3 collective-permute-done.9.refs_1_.refs_7_
  23.6 0.6 collective-permute-start.17
  24.2 2.7 %collective-permute-done.24.refs_0_.refs_6_ = bf16[72,512]{1,0:T(8,128)(2,1)S(1)} collective-permute-done((bf16[72,512]{1,0:T(8,128)(2,1)S(1)}, bf16[72,512]{1,0:T(8,128)(2,1)S(1)}, u32[]{:S(2)}, u32[]{:S(2)}) %collective-permute-start.24) | collective-permute-done | bytes 73760 | tf_op jit(solution)/shard_map/ppermute | solution.py:202
  26.9 1.4 %collective-permute-start.25 = (bf16[72,512]{1,0:T(8,128)(2,1)S(1)}, bf16[72,512]{1,0:T(8,128)(2,1)S(1)}, u32[]{:S(2)}, u32[]{:S(2)}) collective-permute-start(bf16[72,512]{1,0:T(8,128)(2,1)S(1)} %get-tuple-element.53.refs_0_.refs_6_), channel_id=1, source_target_pairs={{0,24},{1,25},{2,26},{3,27},{4,28},{5,29},{6,30},{7,31},{8,16},{9,... | collective-permute-start | bytes 221192 | tf_op jit(solution)/shard_map/ppermute | solution.py:202
  28.4 4.7 %collective-permute-done.25.refs_1_.refs_7_ = bf16[72,512]{1,0:T(8,128)(2,1)S(1)} collective-permute-done((bf16[72,512]{1,0:T(8,128)(2,1)S(1)}, bf16[72,512]{1,0:T(8,128)(2,1)S(1)}, u32[]{:S(2)}, u32[]{:S(2)}) %collective-permute-start.25) | collective-permute-done | bytes 73760 | tf_op jit(solution)/shard_map/ppermute | solution.py:202
  33.1 1.9 %collective-permute-start.18 = (bf16[192,512]{1,0:T(8,128)(2,1)S(1)}, bf16[192,512]{1,0:T(8,128)(2,1)S(1)}, u32[]{:S(2)}, u32[]{:S(2)}) collective-permute-start(bf16[192,512]{1,0:T(8,128)(2,1)S(1)} %get-tuple-element.61), channel_id=1, source_target_pairs={{0,5},{1,4},{2,7},{3,6},{4,1},{5,0},{6,3},{7,2},{8,13},{9,12},{10,... | collective-permute-start | bytes 589832 | tf_op jit(solution)/shard_map/ppermute | solution.py:202
  35.2 5.2 %collective-permute-done.18.refs_7_ = bf16[192,512]{1,0:T(8,128)(2,1)S(1)} collective-permute-done((bf16[192,512]{1,0:T(8,128)(2,1)S(1)}, bf16[192,512]{1,0:T(8,128)(2,1)S(1)}, u32[]{:S(2)}, u32[]{:S(2)}) %collective-permute-start.18) | collective-permute-done | bytes 196640 | tf_op jit(solution)/shard_map/ppermute | solution.py:202
  40.3 1.5 %collective-permute-start.11 = (bf16[128,512]{1,0:T(8,128)(2,1)S(1)}, bf16[128,512]{1,0:T(8,128)(2,1)S(1)}, u32[]{:S(2)}, u32[]{:S(2)}) collective-permute-start(bf16[128,512]{1,0:T(8,128)(2,1)S(1)} %shard_map.130.refs_8_), channel_id=1, source_target_pairs={{0,4},{1,5},{2,6},{3,7},{4,0},{5,1},{6,2},{7,3},{8,12},{9,13},{10,... | collective-permute-start | bytes 393224 | tf_op jit(solution)/shard_map/ppermute | solution.py:202
  41.9 3.4 %collective-permute-start.12 = (bf16[128,512]{1,0:T(8,128)(2,1)S(1)}, bf16[128,512]{1,0:T(8,128)(2,1)S(1)}, u32[]{:S(2)}, u32[]{:S(2)}) collective-permute-start(bf16[128,512]{1,0:T(8,128)(2,1)S(1)} %shard_map.130.refs_8_), channel_id=1, source_target_pairs={{0,5},{1,4},{2,7},{3,6},{4,1},{5,0},{6,3},{7,2},{8,13},{9,12},{10,... | collective-permute-start | bytes 393224 | tf_op jit(solution)/shard_map/ppermute | solution.py:202
  45.6 2.6 %collective-permute-done.12.refs_11_ = bf16[128,512]{1,0:T(8,128)(2,1)S(1)} collective-permute-done((bf16[128,512]{1,0:T(8,128)(2,1)S(1)}, bf16[128,512]{1,0:T(8,128)(2,1)S(1)}, u32[]{:S(2)}, u32[]{:S(2)}) %collective-permute-start.12) | collective-permute-done | bytes 131104 | tf_op jit(solution)/shard_map/ppermute | solution.py:202
  48.2 0.5 collective-permute-start.27
  48.7 1.6 %collective-permute-done.26.refs_9_ = bf16[128,512]{1,0:T(8,128)(2,1)S(1)} collective-permute-done((bf16[128,512]{1,0:T(8,128)(2,1)S(1)}, bf16[128,512]{1,0:T(8,128)(2,1)S(1)}, u32[]{:S(2)}, u32[]{:S(2)}) %collective-permute-start.26) | collective-permute-done | bytes 131104 | tf_op jit(solution)/shard_map/ppermute | solution.py:202
  50.4 0.5 collective-permute-start.22
  50.9 1.3 %collective-permute-start.28 = (bf16[128,512]{1,0:T(8,128)(2,1)S(1)}, bf16[128,512]{1,0:T(8,128)(2,1)S(1)}, u32[]{:S(2)}, u32[]{:S(2)}) collective-permute-start(bf16[128,512]{1,0:T(8,128)(2,1)S(1)} %shard_map.133.refs_8_), channel_id=1, source_target_pairs={{0,5},{1,4},{2,7},{3,6},{4,1},{5,0},{6,3},{7,2},{8,13},{9,12},{10,... | collective-permute-start | bytes 393224 | tf_op jit(solution)/shard_map/ppermute | solution.py:202
  52.2 1.4 %shard_map.131.refs_0_ = bf16[128,384]{1,0:T(8,128)(2,1)S(1)} custom-call(f32[8,8]{1,0:T(8,128)S(1)} %get-tuple-element.40.refs_0_, f32[1,2048]{1,0:T(1,128)S(1)} %bitcast.16, bf16[192,2048]{1,0:T(8,128)(2,1)S(1)} %bitcast.10, bf16[192,2048]{1,0:T(8,128)(2,1)S(1)} %collective-permute-done.4.refs_3_, bf16[192,2048]{1,0:T(8,128)(2,1)S(1)} %bitcast.13, ...), custom_call_target="tpu_custom_call" | custom-call | flops 402653184 | bytes 3924224 | tf_op jit(solution)/shard_map/pallas_call | solution.py:230
  53.6 2.7 %collective-permute-start.13 = (bf16[128,384]{1,0:T(8,128)(2,1)S(1)}, bf16[128,384]{1,0:T(8,128)(2,1)S(1)}, u32[]{:S(2)}, u32[]{:S(2)}) collective-permute-start(bf16[128,384]{1,0:T(8,128)(2,1)S(1)} %shard_map.131.refs_0_), channel_id=1, source_target_pairs={{0,1},{1,0},{2,3},{3,2},{4,5},{5,4},{6,7},{7,6},{8,9},{9,8},{10,11... | collective-permute-start | bytes 294920 | tf_op jit(solution)/shard_map/ppermute | solution.py:202
  56.3 1.2 %collective-permute-done.28.refs_11_ = bf16[128,512]{1,0:T(8,128)(2,1)S(1)} collective-permute-done((bf16[128,512]{1,0:T(8,128)(2,1)S(1)}, bf16[128,512]{1,0:T(8,128)(2,1)S(1)}, u32[]{:S(2)}, u32[]{:S(2)}) %collective-permute-start.28) | collective-permute-done | bytes 131104 | tf_op jit(solution)/shard_map/ppermute | solution.py:202
  57.5 1.4 %collective-permute-start.14 = (bf16[128,384]{1,0:T(8,128)(2,1)S(1)}, bf16[128,384]{1,0:T(8,128)(2,1)S(1)}, u32[]{:S(2)}, u32[]{:S(2)}) collective-permute-start(bf16[128,384]{1,0:T(8,128)(2,1)S(1)} %shard_map.131.refs_0_), channel_id=1, source_target_pairs={{0,4},{1,5},{2,6},{3,7},{4,0},{5,1},{6,2},{7,3},{8,12},{9,13},{10,... | collective-permute-start | bytes 294920 | tf_op jit(solution)/shard_map/ppermute | solution.py:202
  58.9 2.0 %collective-permute-start.15 = (bf16[128,384]{1,0:T(8,128)(2,1)S(1)}, bf16[128,384]{1,0:T(8,128)(2,1)S(1)}, u32[]{:S(2)}, u32[]{:S(2)}) collective-permute-start(bf16[128,384]{1,0:T(8,128)(2,1)S(1)} %shard_map.131.refs_0_), channel_id=1, source_target_pairs={{0,5},{1,4},{2,7},{3,6},{4,1},{5,0},{6,3},{7,2},{8,13},{9,12},{10,... | collective-permute-start | bytes 294920 | tf_op jit(solution)/shard_map/ppermute | solution.py:202
  61.0 1.4 %shard_map.134.refs_0_ = bf16[128,384]{1,0:T(8,128)(2,1)S(1)} custom-call(f32[8,8]{1,0:T(8,128)S(1)} %get-tuple-element.40.refs_0_, f32[1,2048]{1,0:T(1,128)S(1)} %bitcast.17, bf16[192,2048]{1,0:T(8,128)(2,1)S(1)} %bitcast.11, bf16[192,2048]{1,0:T(8,128)(2,1)S(1)} %collective-permute-done.4.refs_3_, bf16[192,2048]{1,0:T(8,128)(2,1)S(1)} %bitcast.14, ...), custom_call_target="tpu_custom_call" | custom-call | flops 402653184 | bytes 3924224 | tf_op jit(solution)/shard_map/pallas_call | solution.py:230
  62.5 1.4 %collective-permute-start.30 = (bf16[128,384]{1,0:T(8,128)(2,1)S(1)}, bf16[128,384]{1,0:T(8,128)(2,1)S(1)}, u32[]{:S(2)}, u32[]{:S(2)}) collective-permute-start(bf16[128,384]{1,0:T(8,128)(2,1)S(1)} %shard_map.134.refs_0_), channel_id=1, source_target_pairs={{0,4},{1,5},{2,6},{3,7},{4,0},{5,1},{6,2},{7,3},{8,12},{9,13},{10,... | collective-permute-start | bytes 294920 | tf_op jit(solution)/shard_map/ppermute | solution.py:202
  63.9 2.0 %collective-permute-start.31 = (bf16[128,384]{1,0:T(8,128)(2,1)S(1)}, bf16[128,384]{1,0:T(8,128)(2,1)S(1)}, u32[]{:S(2)}, u32[]{:S(2)}) collective-permute-start(bf16[128,384]{1,0:T(8,128)(2,1)S(1)} %shard_map.134.refs_0_), channel_id=1, source_target_pairs={{0,5},{1,4},{2,7},{3,6},{4,1},{5,0},{6,3},{7,2},{8,13},{9,12},{10,... | collective-permute-start | bytes 294920 | tf_op jit(solution)/shard_map/ppermute | solution.py:202
  65.9 0.4 shard_map.132
  66.5 0.6 collective-permute-done.29.refs_1_
  67.1 0.3 collective-permute-done.30.refs_2_
  67.4 2.0 %collective-permute-done.31.refs_3_ = bf16[128,384]{1,0:T(8,128)(2,1)S(1)} collective-permute-done((bf16[128,384]{1,0:T(8,128)(2,1)S(1)}, bf16[128,384]{1,0:T(8,128)(2,1)S(1)}, u32[]{:S(2)}, u32[]{:S(2)}) %collective-permute-start.31) | collective-permute-done | bytes 98336 | tf_op jit(solution)/shard_map/ppermute | solution.py:202
  69.4 0.4 shard_map.135
  69.9 1.4 %collective-permute-start.32 = (bf16[64,512]{1,0:T(8,128)(2,1)S(1)}, bf16[64,512]{1,0:T(8,128)(2,1)S(1)}, u32[]{:S(2)}, u32[]{:S(2)}) collective-permute-start(bf16[64,512]{1,0:T(8,128)(2,1)S(1)} %get-tuple-element.65), channel_id=1, source_target_pairs={{0,16},{1,17},{2,18},{3,19},{4,20},{5,21},{6,22},{7,23},{8,24},{9,... | collective-permute-start | bytes 196616 | tf_op jit(solution)/shard_map/ppermute | solution.py:202
  71.3 0.4 collective-permute-start.33
  71.7 3.4 %collective-permute-done.32.refs_2_ = bf16[64,512]{1,0:T(8,128)(2,1)S(1)} collective-permute-done((bf16[64,512]{1,0:T(8,128)(2,1)S(1)}, bf16[64,512]{1,0:T(8,128)(2,1)S(1)}, u32[]{:S(2)}, u32[]{:S(2)}) %collective-permute-start.32) | collective-permute-done | bytes 65568 | tf_op jit(solution)/shard_map/ppermute | solution.py:202
  75.1 2.2 %collective-permute-done.33.refs_3_ = bf16[64,512]{1,0:T(8,128)(2,1)S(1)} collective-permute-done((bf16[64,512]{1,0:T(8,128)(2,1)S(1)}, bf16[64,512]{1,0:T(8,128)(2,1)S(1)}, u32[]{:S(2)}, u32[]{:S(2)}) %collective-permute-start.33) | collective-permute-done | bytes 65568 | tf_op jit(solution)/shard_map/ppermute | solution.py:202
  77.4 1.2 %collective-permute-done.34.other = bf16[64,256]{1,0:T(8,128)(2,1)S(1)} collective-permute-done((bf16[64,256]{1,0:T(8,128)(2,1)S(1)}, bf16[64,256]{1,0:T(8,128)(2,1)S(1)}, u32[]{:S(2)}, u32[]{:S(2)}) %collective-permute-start.34) | collective-permute-done | bytes 32800 | tf_op jit(solution)/shard_map/ppermute | solution.py:202
  78.6 0.6 shard_map.137
  (48 shorter events, 1.9 us)
Async XLA Ops:
  0.0 9.6 %copy-start.2 = (bf16[128,2048]{1,0:T(8,128)(2,1)S(1)}, bf16[128,2048]{1,0:T(8,128)(2,1)}, u32[]{:S(2)}) copy-start(bf16[128,2048]{1,0:T(8,128)(2,1)} %refs_6_.1) | copy-start | bytes 1572868
  2.7 6.9 %collective-permute-start.3 = (bf16[256,2048]{1,0:T(8,128)(2,1)S(1)}, bf16[256,2048]{1,0:T(8,128)(2,1)S(1)}, u32[]{:S(2)}, u32[]{:S(2)}) collective-permute-start(bf16[256,2048]{1,0:T(8,128)(2,1)S(1)} %get-tuple-element.45.refs_4_), channel_id=1, source_target_pairs={{0,2},{1,3},{2,0},{3,1},{4,6},{5,7},{6,4},{7,5},{8,10},{9,11},{10,... | collective-permute-start | bytes 3145736 | tf_op jit(solution)/shard_map/ppermute | solution.py:202
  3.2 2.7 %copy-start.5 = (f32[128,8]{0,1:T(8,128)S(1)}, f32[128,8]{0,1:T(8,128)}, u32[]{:S(2)}) copy-start(f32[128,8]{0,1:T(8,128)} %param.21) | copy-start | bytes 12292
  3.2 2.7 %copy-start.4 = (s32[128,8]{0,1:T(8,128)S(1)}, s32[128,8]{0,1:T(8,128)}, u32[]{:S(2)}) copy-start(s32[128,8]{0,1:T(8,128)} %param.20) | copy-start | bytes 12292
  3.2 4.0 %collective-permute-start = (bf16[32,256]{1,0:T(8,128)(2,1)S(1)}, bf16[32,256]{1,0:T(8,128)(2,1)S(1)}, u32[]{:S(2)}, u32[]{:S(2)}) collective-permute-start(bf16[32,256]{1,0:T(8,128)(2,1)S(1)} %get-tuple-element.37), channel_id=1, source_target_pairs={{0,3},{1,2},{2,1},{3,0},{4,7},{5,6},{6,5},{7,4},{8,11},{9,10},{10,... | collective-permute-start | bytes 49160 | tf_op jit(solution)/shard_map/ppermute | solution.py:202
  5.8 3.7 %collective-permute-start.1 = (bf16[32,256]{1,0:T(8,128)(2,1)S(1)}, bf16[32,256]{1,0:T(8,128)(2,1)S(1)}, u32[]{:S(2)}, u32[]{:S(2)}) collective-permute-start(bf16[32,256]{1,0:T(8,128)(2,1)S(1)} %get-tuple-element.42), channel_id=1, source_target_pairs={{0,1},{1,0},{2,3},{3,2},{4,5},{5,4},{6,7},{7,6},{8,9},{9,8},{10,11... | collective-permute-start | bytes 49160 | tf_op jit(solution)/shard_map/ppermute | solution.py:202
  5.9 3.7 %collective-permute-start.2 = (bf16[32,256]{1,0:T(8,128)(2,1)S(1)}, bf16[32,256]{1,0:T(8,128)(2,1)S(1)}, u32[]{:S(2)}, u32[]{:S(2)}) collective-permute-start(bf16[32,256]{1,0:T(8,128)(2,1)S(1)} %get-tuple-element.43), channel_id=1, source_target_pairs={{0,2},{1,3},{2,0},{3,1},{4,6},{5,7},{6,4},{7,5},{8,10},{9,11},{10,... | collective-permute-start | bytes 49160 | tf_op jit(solution)/shard_map/ppermute | solution.py:202
  6.0 0.7 copy-start.6
  9.6 1.1 %copy-start = (bf16[1,2048,192]{1,2,0:T(8,128)(2,1)S(1)}, bf16[1,2048,192]{1,2,0:T(8,128)(2,1)}, u32[]{:S(2)}) copy-start(bf16[1,2048,192]{1,2,0:T(8,128)(2,1)} %param.23) | copy-start | bytes 2359300
  9.6 1.4 %copy-start.1 = (bf16[1,2048,192]{1,2,0:T(8,128)(2,1)S(1)}, bf16[1,2048,192]{1,2,0:T(8,128)(2,1)}, u32[]{:S(2)}) copy-start(bf16[1,2048,192]{1,2,0:T(8,128)(2,1)} %param.24) | copy-start | bytes 2359300
  10.7 8.1 %copy-start.3 = (f32[2048]{0:T(1024)S(1)}, f32[2048]{0:T(1024)}, u32[]{:S(2)}) copy-start(f32[2048]{0:T(1024)} %param.19) | copy-start | bytes 24580
  10.7 39.6 %collective-permute-start.4 = (bf16[192,2048]{1,0:T(8,128)(2,1)S(1)}, bf16[192,2048]{1,0:T(8,128)(2,1)S(1)}, u32[]{:S(2)}, u32[]{:S(2)}) collective-permute-start(bf16[192,2048]{1,0:T(8,128)(2,1)S(1)} %bitcast.9), channel_id=1, source_target_pairs={{0,2},{1,3},{2,0},{3,1},{4,6},{5,7},{6,4},{7,5},{8,10},{9,11},{10,... | collective-permute-start | bytes 2359304 | tf_op jit(solution)/shard_map/ppermute | solution.py:202
  11.0 39.9 %collective-permute-start.5 = (bf16[192,2048]{1,0:T(8,128)(2,1)S(1)}, bf16[192,2048]{1,0:T(8,128)(2,1)S(1)}, u32[]{:S(2)}, u32[]{:S(2)}) collective-permute-start(bf16[192,2048]{1,0:T(8,128)(2,1)S(1)} %bitcast.12), channel_id=1, source_target_pairs={{0,2},{1,3},{2,0},{3,1},{4,6},{5,7},{6,4},{7,5},{8,10},{9,11},{10,... | collective-permute-start | bytes 2359304 | tf_op jit(solution)/shard_map/ppermute | solution.py:202
  11.2 4.5 %collective-permute-start.6 = (bf16[64,512]{1,0:T(8,128)(2,1)S(1)}, bf16[64,512]{1,0:T(8,128)(2,1)S(1)}, u32[]{:S(2)}, u32[]{:S(2)}) collective-permute-start(bf16[64,512]{1,0:T(8,128)(2,1)S(1)} %get-tuple-element.46), channel_id=1, source_target_pairs={{0,1},{1,0},{2,3},{3,2},{4,5},{5,4},{6,7},{7,6},{8,9},{9,8},{10,11... | collective-permute-start | bytes 196616 | tf_op jit(solution)/shard_map/ppermute | solution.py:202
  11.4 5.1 %collective-permute-start.7 = (bf16[64,512]{1,0:T(8,128)(2,1)S(1)}, bf16[64,512]{1,0:T(8,128)(2,1)S(1)}, u32[]{:S(2)}, u32[]{:S(2)}) collective-permute-start(bf16[64,512]{1,0:T(8,128)(2,1)S(1)} %get-tuple-element.50), channel_id=1, source_target_pairs={{0,4},{1,5},{2,6},{3,7},{4,0},{5,1},{6,2},{7,3},{8,12},{9,13},{10,... | collective-permute-start | bytes 196616 | tf_op jit(solution)/shard_map/ppermute | solution.py:202
  13.3 5.5 %collective-permute-start.8 = (bf16[64,512]{1,0:T(8,128)(2,1)S(1)}, bf16[64,512]{1,0:T(8,128)(2,1)S(1)}, u32[]{:S(2)}, u32[]{:S(2)}) collective-permute-start(bf16[64,512]{1,0:T(8,128)(2,1)S(1)} %get-tuple-element.51), channel_id=1, source_target_pairs={{0,5},{1,4},{2,7},{3,6},{4,1},{5,0},{6,3},{7,2},{8,13},{9,12},{10,... | collective-permute-start | bytes 196616 | tf_op jit(solution)/shard_map/ppermute | solution.py:202
  15.7 19.3 %collective-permute-start.16 = (bf16[192,512]{1,0:T(8,128)(2,1)S(1)}, bf16[192,512]{1,0:T(8,128)(2,1)S(1)}, u32[]{:S(2)}, u32[]{:S(2)}) collective-permute-start(bf16[192,512]{1,0:T(8,128)(2,1)S(1)} %get-tuple-element.59), channel_id=1, source_target_pairs={{0,1},{1,0},{2,3},{3,2},{4,5},{5,4},{6,7},{7,6},{8,9},{9,8},{10,11... | collective-permute-start | bytes 589832 | tf_op jit(solution)/shard_map/ppermute | solution.py:202
  19.0 4.5 %collective-permute-start.9 = (bf16[72,512]{1,0:T(8,128)(2,1)S(1)}, bf16[72,512]{1,0:T(8,128)(2,1)S(1)}, u32[]{:S(2)}, u32[]{:S(2)}) collective-permute-start(bf16[72,512]{1,0:T(8,128)(2,1)S(1)} %get-tuple-element.53.refs_0_.refs_6_), channel_id=1, source_target_pairs={{0,8},{1,9},{2,10},{3,11},{4,12},{5,13},{6,14},{7,15},{8,0},{9,1},... | collective-permute-start | bytes 221192 | tf_op jit(solution)/shard_map/ppermute | solution.py:202
  20.6 6.3 %collective-permute-start.24 = (bf16[72,512]{1,0:T(8,128)(2,1)S(1)}, bf16[72,512]{1,0:T(8,128)(2,1)S(1)}, u32[]{:S(2)}, u32[]{:S(2)}) collective-permute-start(bf16[72,512]{1,0:T(8,128)(2,1)S(1)} %get-tuple-element.53.refs_0_.refs_6_), channel_id=1, source_target_pairs={{0,16},{1,17},{2,18},{3,19},{4,20},{5,21},{6,22},{7,23},{8,24},{9,... | collective-permute-start | bytes 221192 | tf_op jit(solution)/shard_map/ppermute | solution.py:202
  23.6 11.5 %collective-permute-start.17 = (bf16[192,512]{1,0:T(8,128)(2,1)S(1)}, bf16[192,512]{1,0:T(8,128)(2,1)S(1)}, u32[]{:S(2)}, u32[]{:S(2)}) collective-permute-start(bf16[192,512]{1,0:T(8,128)(2,1)S(1)} %get-tuple-element.60), channel_id=1, source_target_pairs={{0,4},{1,5},{2,6},{3,7},{4,0},{5,1},{6,2},{7,3},{8,12},{9,13},{10,... | collective-permute-start | bytes 589832 | tf_op jit(solution)/shard_map/ppermute | solution.py:202
  26.9 6.2 %collective-permute-start.25 = (bf16[72,512]{1,0:T(8,128)(2,1)S(1)}, bf16[72,512]{1,0:T(8,128)(2,1)S(1)}, u32[]{:S(2)}, u32[]{:S(2)}) collective-permute-start(bf16[72,512]{1,0:T(8,128)(2,1)S(1)} %get-tuple-element.53.refs_0_.refs_6_), channel_id=1, source_target_pairs={{0,24},{1,25},{2,26},{3,27},{4,28},{5,29},{6,30},{7,31},{8,16},{9,... | collective-permute-start | bytes 221192 | tf_op jit(solution)/shard_map/ppermute | solution.py:202
  33.1 7.3 %collective-permute-start.18 = (bf16[192,512]{1,0:T(8,128)(2,1)S(1)}, bf16[192,512]{1,0:T(8,128)(2,1)S(1)}, u32[]{:S(2)}, u32[]{:S(2)}) collective-permute-start(bf16[192,512]{1,0:T(8,128)(2,1)S(1)} %get-tuple-element.61), channel_id=1, source_target_pairs={{0,5},{1,4},{2,7},{3,6},{4,1},{5,0},{6,3},{7,2},{8,13},{9,12},{10,... | collective-permute-start | bytes 589832 | tf_op jit(solution)/shard_map/ppermute | solution.py:202
  35.0 6.9 %collective-permute-start.19 = (bf16[192,512]{1,0:T(8,128)(2,1)S(1)}, bf16[192,512]{1,0:T(8,128)(2,1)S(1)}, u32[]{:S(2)}, u32[]{:S(2)}) collective-permute-start(bf16[192,512]{1,0:T(8,128)(2,1)S(1)} %get-tuple-element.58.refs_4_), channel_id=1, source_target_pairs={{0,2},{1,3},{2,0},{3,1},{4,6},{5,7},{6,4},{7,5},{8,10},{9,11},{10,... | collective-permute-start | bytes 589832 | tf_op jit(solution)/shard_map/ppermute | solution.py:202
  35.0 10.3 %collective-permute-start.10 = (bf16[128,512]{1,0:T(8,128)(2,1)S(1)}, bf16[128,512]{1,0:T(8,128)(2,1)S(1)}, u32[]{:S(2)}, u32[]{:S(2)}) collective-permute-start(bf16[128,512]{1,0:T(8,128)(2,1)S(1)} %shard_map.130.refs_8_), channel_id=1, source_target_pairs={{0,1},{1,0},{2,3},{3,2},{4,5},{5,4},{6,7},{7,6},{8,9},{9,8},{10,11... | collective-permute-start | bytes 393224 | tf_op jit(solution)/shard_map/ppermute | solution.py:202
  40.3 5.3 %collective-permute-start.11 = (bf16[128,512]{1,0:T(8,128)(2,1)S(1)}, bf16[128,512]{1,0:T(8,128)(2,1)S(1)}, u32[]{:S(2)}, u32[]{:S(2)}) collective-permute-start(bf16[128,512]{1,0:T(8,128)(2,1)S(1)} %shard_map.130.refs_8_), channel_id=1, source_target_pairs={{0,4},{1,5},{2,6},{3,7},{4,0},{5,1},{6,2},{7,3},{8,12},{9,13},{10,... | collective-permute-start | bytes 393224 | tf_op jit(solution)/shard_map/ppermute | solution.py:202
  41.9 6.4 %collective-permute-start.12 = (bf16[128,512]{1,0:T(8,128)(2,1)S(1)}, bf16[128,512]{1,0:T(8,128)(2,1)S(1)}, u32[]{:S(2)}, u32[]{:S(2)}) collective-permute-start(bf16[128,512]{1,0:T(8,128)(2,1)S(1)} %shard_map.130.refs_8_), channel_id=1, source_target_pairs={{0,5},{1,4},{2,7},{3,6},{4,1},{5,0},{6,3},{7,2},{8,13},{9,12},{10,... | collective-permute-start | bytes 393224 | tf_op jit(solution)/shard_map/ppermute | solution.py:202
  45.3 5.0 %collective-permute-start.26 = (bf16[128,512]{1,0:T(8,128)(2,1)S(1)}, bf16[128,512]{1,0:T(8,128)(2,1)S(1)}, u32[]{:S(2)}, u32[]{:S(2)}) collective-permute-start(bf16[128,512]{1,0:T(8,128)(2,1)S(1)} %shard_map.133.refs_8_), channel_id=1, source_target_pairs={{0,1},{1,0},{2,3},{3,2},{4,5},{5,4},{6,7},{7,6},{8,9},{9,8},{10,11... | collective-permute-start | bytes 393224 | tf_op jit(solution)/shard_map/ppermute | solution.py:202
  45.6 13.3 %collective-permute-start.20 = (bf16[192,512]{1,0:T(8,128)(2,1)S(1)}, bf16[192,512]{1,0:T(8,128)(2,1)S(1)}, u32[]{:S(2)}, u32[]{:S(2)}) collective-permute-start(bf16[192,512]{1,0:T(8,128)(2,1)S(1)} %collective-permute-done.16.refs_5_), channel_id=1, source_target_pairs={{0,2},{1,3},{2,0},{3,1},{4,6},{5,7},{6,4},{7,5},{8,10},{9,11},{10,... | collective-permute-start | bytes 589832 | tf_op jit(solution)/shard_map/ppermute | solution.py:202
  48.2 5.3 %collective-permute-start.27 = (bf16[128,512]{1,0:T(8,128)(2,1)S(1)}, bf16[128,512]{1,0:T(8,128)(2,1)S(1)}, u32[]{:S(2)}, u32[]{:S(2)}) collective-permute-start(bf16[128,512]{1,0:T(8,128)(2,1)S(1)} %shard_map.133.refs_8_), channel_id=1, source_target_pairs={{0,4},{1,5},{2,6},{3,7},{4,0},{5,1},{6,2},{7,3},{8,12},{9,13},{10,... | collective-permute-start | bytes 393224 | tf_op jit(solution)/shard_map/ppermute | solution.py:202
  50.3 12.0 %collective-permute-start.21 = (bf16[192,512]{1,0:T(8,128)(2,1)S(1)}, bf16[192,512]{1,0:T(8,128)(2,1)S(1)}, u32[]{:S(2)}, u32[]{:S(2)}) collective-permute-start(bf16[192,512]{1,0:T(8,128)(2,1)S(1)} %collective-permute-done.17.refs_6_), channel_id=1, source_target_pairs={{0,2},{1,3},{2,0},{3,1},{4,6},{5,7},{6,4},{7,5},{8,10},{9,11},{10,... | collective-permute-start | bytes 589832 | tf_op jit(solution)/shard_map/ppermute | solution.py:202
  50.4 12.1 %collective-permute-start.22 = (bf16[192,512]{1,0:T(8,128)(2,1)S(1)}, bf16[192,512]{1,0:T(8,128)(2,1)S(1)}, u32[]{:S(2)}, u32[]{:S(2)}) collective-permute-start(bf16[192,512]{1,0:T(8,128)(2,1)S(1)} %collective-permute-done.18.refs_7_), channel_id=1, source_target_pairs={{0,2},{1,3},{2,0},{3,1},{4,6},{5,7},{6,4},{7,5},{8,10},{9,11},{10,... | collective-permute-start | bytes 589832 | tf_op jit(solution)/shard_map/ppermute | solution.py:202
  50.9 6.6 %collective-permute-start.28 = (bf16[128,512]{1,0:T(8,128)(2,1)S(1)}, bf16[128,512]{1,0:T(8,128)(2,1)S(1)}, u32[]{:S(2)}, u32[]{:S(2)}) collective-permute-start(bf16[128,512]{1,0:T(8,128)(2,1)S(1)} %shard_map.133.refs_8_), channel_id=1, source_target_pairs={{0,5},{1,4},{2,7},{3,6},{4,1},{5,0},{6,3},{7,2},{8,13},{9,12},{10,... | collective-permute-start | bytes 393224 | tf_op jit(solution)/shard_map/ppermute | solution.py:202
  53.6 10.3 %collective-permute-start.13 = (bf16[128,384]{1,0:T(8,128)(2,1)S(1)}, bf16[128,384]{1,0:T(8,128)(2,1)S(1)}, u32[]{:S(2)}, u32[]{:S(2)}) collective-permute-start(bf16[128,384]{1,0:T(8,128)(2,1)S(1)} %shard_map.131.refs_0_), channel_id=1, source_target_pairs={{0,1},{1,0},{2,3},{3,2},{4,5},{5,4},{6,7},{7,6},{8,9},{9,8},{10,11... | collective-permute-start | bytes 294920 | tf_op jit(solution)/shard_map/ppermute | solution.py:202
  57.5 8.5 %collective-permute-start.14 = (bf16[128,384]{1,0:T(8,128)(2,1)S(1)}, bf16[128,384]{1,0:T(8,128)(2,1)S(1)}, u32[]{:S(2)}, u32[]{:S(2)}) collective-permute-start(bf16[128,384]{1,0:T(8,128)(2,1)S(1)} %shard_map.131.refs_0_), channel_id=1, source_target_pairs={{0,4},{1,5},{2,6},{3,7},{4,0},{5,1},{6,2},{7,3},{8,12},{9,13},{10,... | collective-permute-start | bytes 294920 | tf_op jit(solution)/shard_map/ppermute | solution.py:202
  58.9 7.0 %collective-permute-start.15 = (bf16[128,384]{1,0:T(8,128)(2,1)S(1)}, bf16[128,384]{1,0:T(8,128)(2,1)S(1)}, u32[]{:S(2)}, u32[]{:S(2)}) collective-permute-start(bf16[128,384]{1,0:T(8,128)(2,1)S(1)} %shard_map.131.refs_0_), channel_id=1, source_target_pairs={{0,5},{1,4},{2,7},{3,6},{4,1},{5,0},{6,3},{7,2},{8,13},{9,12},{10,... | collective-permute-start | bytes 294920 | tf_op jit(solution)/shard_map/ppermute | solution.py:202
  62.4 4.7 %collective-permute-start.29 = (bf16[128,384]{1,0:T(8,128)(2,1)S(1)}, bf16[128,384]{1,0:T(8,128)(2,1)S(1)}, u32[]{:S(2)}, u32[]{:S(2)}) collective-permute-start(bf16[128,384]{1,0:T(8,128)(2,1)S(1)} %shard_map.134.refs_0_), channel_id=1, source_target_pairs={{0,1},{1,0},{2,3},{3,2},{4,5},{5,4},{6,7},{7,6},{8,9},{9,8},{10,11... | collective-permute-start | bytes 294920 | tf_op jit(solution)/shard_map/ppermute | solution.py:202
  62.5 4.9 %collective-permute-start.30 = (bf16[128,384]{1,0:T(8,128)(2,1)S(1)}, bf16[128,384]{1,0:T(8,128)(2,1)S(1)}, u32[]{:S(2)}, u32[]{:S(2)}) collective-permute-start(bf16[128,384]{1,0:T(8,128)(2,1)S(1)} %shard_map.134.refs_0_), channel_id=1, source_target_pairs={{0,4},{1,5},{2,6},{3,7},{4,0},{5,1},{6,2},{7,3},{8,12},{9,13},{10,... | collective-permute-start | bytes 294920 | tf_op jit(solution)/shard_map/ppermute | solution.py:202
  63.9 5.5 %collective-permute-start.31 = (bf16[128,384]{1,0:T(8,128)(2,1)S(1)}, bf16[128,384]{1,0:T(8,128)(2,1)S(1)}, u32[]{:S(2)}, u32[]{:S(2)}) collective-permute-start(bf16[128,384]{1,0:T(8,128)(2,1)S(1)} %shard_map.134.refs_0_), channel_id=1, source_target_pairs={{0,5},{1,4},{2,7},{3,6},{4,1},{5,0},{6,3},{7,2},{8,13},{9,12},{10,... | collective-permute-start | bytes 294920 | tf_op jit(solution)/shard_map/ppermute | solution.py:202
  66.4 5.3 %collective-permute-start.23 = (bf16[64,512]{1,0:T(8,128)(2,1)S(1)}, bf16[64,512]{1,0:T(8,128)(2,1)S(1)}, u32[]{:S(2)}, u32[]{:S(2)}) collective-permute-start(bf16[64,512]{1,0:T(8,128)(2,1)S(1)} %get-tuple-element.64), channel_id=1, source_target_pairs={{0,8},{1,9},{2,10},{3,11},{4,12},{5,13},{6,14},{7,15},{8,0},{9,1},... | collective-permute-start | bytes 196616 | tf_op jit(solution)/shard_map/ppermute | solution.py:202
  69.9 5.2 %collective-permute-start.32 = (bf16[64,512]{1,0:T(8,128)(2,1)S(1)}, bf16[64,512]{1,0:T(8,128)(2,1)S(1)}, u32[]{:S(2)}, u32[]{:S(2)}) collective-permute-start(bf16[64,512]{1,0:T(8,128)(2,1)S(1)} %get-tuple-element.65), channel_id=1, source_target_pairs={{0,16},{1,17},{2,18},{3,19},{4,20},{5,21},{6,22},{7,23},{8,24},{9,... | collective-permute-start | bytes 196616 | tf_op jit(solution)/shard_map/ppermute | solution.py:202
  71.3 6.1 %collective-permute-start.33 = (bf16[64,512]{1,0:T(8,128)(2,1)S(1)}, bf16[64,512]{1,0:T(8,128)(2,1)S(1)}, u32[]{:S(2)}, u32[]{:S(2)}) collective-permute-start(bf16[64,512]{1,0:T(8,128)(2,1)S(1)} %get-tuple-element.66), channel_id=1, source_target_pairs={{0,24},{1,25},{2,26},{3,27},{4,28},{5,29},{6,30},{7,31},{8,16},{9,... | collective-permute-start | bytes 196616 | tf_op jit(solution)/shard_map/ppermute | solution.py:202
  77.4 1.3 %collective-permute-start.34 = (bf16[64,256]{1,0:T(8,128)(2,1)S(1)}, bf16[64,256]{1,0:T(8,128)(2,1)S(1)}, u32[]{:S(2)}, u32[]{:S(2)}) collective-permute-start(bf16[64,256]{1,0:T(8,128)(2,1)S(1)} %get-tuple-element.68), channel_id=1, source_target_pairs={{0,2},{1,3},{2,0},{3,1},{4,6},{5,7},{6,4},{7,5},{8,10},{9,11},{10,... | collective-permute-start | bytes 98312 | tf_op jit(solution)/shard_map/ppermute | solution.py:202

commit v2 on v1

--- a/solution.py
+++ b/solution.py
@@ -363,13 +363,29 @@
     )(*(pltpu.with_memory_space_constraint(arg, pltpu.HBM) for arg in args))
 
 
-def routes_kernel(slots, ids, gates, shares, serves):
+def routes_kernel(rows, slots, ids, gates, gate, up, tail, serves, weights, sems):
+    hidden = gate.shape[0]
+    copies_in = [
+        pltpu.make_async_copy(ref, weights.at[index * hidden : (index + 1) * hidden, :], sems.at[index])
+        for index, ref in enumerate((gate, up))
+    ]
+    for copy in copies_in:
+        copy.start()
     probs_top = gates[...] / jnp.sum(gates[...], axis=0, keepdims=True)
-    n_experts = shares.shape[0]
-    for expert in range(n_experts):
-        shares[expert : expert + 1, :] = jnp.sum(
-            jnp.where(ids[...] == expert, probs_top, 0.0), axis=0, keepdims=True
-        )
+    n_experts, width = tail.shape
+    shares = jnp.concatenate(
+        [
+            jnp.sum(jnp.where(ids[...] == expert, probs_top, 0.0), axis=0, keepdims=True)
+            for expert in range(n_experts)
+        ],
+        axis=0,
+    )
+    chosen = own_tokens(rows, shares.shape[1], place()[2])
+    table = nt_dot(shares, chosen, precision=lax.Precision.HIGHEST)
+    high = table.astype(BF16)
+    low = (table - high.astype(F32)).astype(BF16)
+    rest = jnp.zeros((n_experts, width - 2 * rows), BF16)
+    tail[...] = jnp.concatenate([high, low, rest], axis=1)
     req, row, core, _ = place()
     n_kvh = lax.axis_size("kvh")
     lane = lax.broadcasted_iota(jnp.int32, (1, n_experts), 1)
@@ -386,6 +402,8 @@
         for d_req in range(n_req):
             chosen = jnp.where(lax.rem(req ^ d_req, copies) == rank, expert, -1)
             serves[2 * d_req + index : 2 * d_req + index + 1, :] = (lane == chosen).astype(F32)
+    for copy in copies_in:
+        copy.wait()
 
 
 def columns_of(d_exp, d_row, index, block):
@@ -427,10 +445,9 @@
 
 
 def mixed_kernel(count, *refs):
-    own, others, (gain, shares, mixed, sent) = refs[0], refs[1:count], refs[count:]
+    own, others, (gain, tail, mixed, sent) = refs[0], refs[1:count], refs[count:]
     rows = own.shape[0]
     block = own.shape[1] // 2
-    _, _, core, _ = place()
     for index in range(2):
         here = slice(index * block, (index + 1) * block)
         total = own[:, here]
@@ -439,12 +456,7 @@
         mixed[:, here] = total
         scale = gain[:, pl.ds(columns_of(0, 0, index, block), block)]
         sent[:rows, here] = (total * scale).astype(BF16)
-    chosen = own_tokens(rows, shares.shape[1], core)
-    table = nt_dot(shares[...], chosen, precision=lax.Precision.HIGHEST)
-    high = table.astype(BF16)
-    low = (table - high.astype(F32)).astype(BF16)
-    rest = jnp.zeros((table.shape[0], 2 * block - 2 * rows), BF16)
-    sent[rows:, :] = jnp.concatenate([high, low, rest], axis=1)
+    sent[rows:, :] = tail[...]
 
 
 def joined_kernel(*refs):
@@ -456,26 +468,31 @@
 
 def expert_kernel(chips, groups, *refs):
     serves, gain = refs[0], refs[1]
-    weights = refs[2:6]
-    sents = refs[6 : 6 + len(groups)]
-    parts = refs[6 + len(groups) : -1]
+    weights = refs[2:4]
+    sents = refs[4 : 4 + len(groups)]
+    parts = refs[4 + len(groups) : -1]
     act_ref = refs[-1]
     rows = parts[0].shape[0] // len(groups)
     block = parts[0].shape[1] // 2
-    hidden, d_model = weights[0].shape
-    gates = None
-    squares = None
-    for part_ref, (d_exp, d_row) in zip(parts, chips, strict=True):
-        for index in range(2):
-            where = pl.ds(columns_of(d_exp, d_row, index, block), block)
-            part = part_ref[:, index * block : (index + 1) * block]
-            weight = jnp.concatenate([ref[:, where] for ref in weights], axis=0)
-            product = nt_dot(part, weight)
-            plain = part.astype(F32)
-            scale = gain[:, where]
-            square = jnp.sum(plain * plain * (1.0 / (scale * scale)), axis=1, keepdims=True)
-            gates = product if gates is None else gates + product
-            squares = square if squares is None else squares + square
+    hidden, d_model = weights[0].shape[0] // 2, weights[0].shape[1]
+    spots = [
+        pl.ds(columns_of(d_exp, d_row, index, block), block)
+        for d_exp, d_row in chips
+        for index in range(2)
+    ]
+    part = jnp.concatenate([ref[...] for ref in parts], axis=1)
+    weight = jnp.concatenate(
+        [
+            jnp.concatenate([ref[half * hidden : (half + 1) * hidden, at] for at in spots], axis=1)
+            for half in range(2)
+            for ref in weights
+        ],
+        axis=0,
+    )
+    gates = nt_dot(part, weight)
+    gains = jnp.concatenate([gain[:, at] for at in spots], axis=1)
+    plain = part.astype(F32)
+    squares = jnp.sum(plain * plain * (1.0 / (gains * gains)), axis=1, keepdims=True)
     scale = lax.rsqrt(squares / d_model + 1e-06)
     gate = gates[:, : 2 * hidden] * scale
     up = gates[:, 2 * hidden :] * scale
@@ -499,15 +516,16 @@
 
 
 def combine_kernel(count, groups, *refs):
-    acts, near, far = refs[:count], refs[count : 2 * count], refs[2 * count : 3 * count]
-    rest = refs[3 * count :]
+    acts, (near, far), rest = refs[:count], refs[count : count + 2], refs[count + 2 :]
     mixed = None
     if 0 in groups:
         mixed, rest = rest[0], rest[1:]
     rows = acts[0].shape[0] // len(groups)
     total = None
-    for act, low, high in zip(acts, near, far, strict=True):
-        product = nn_dot(act[...], jnp.concatenate([low[...], high[...]], axis=0))
+    hidden = near.shape[0] // count
+    for index, act in enumerate(acts):
+        here = slice(index * hidden, (index + 1) * hidden)
+        product = nn_dot(act[...], jnp.concatenate([near[here, :], far[here, :]], axis=0))
         total = product if total is None else total + product
     for index, (d_req, out) in enumerate(zip(groups, rest, strict=True)):
         part = total[index * rows : (index + 1) * rows]
@@ -534,6 +552,35 @@
         for half in range(2):
             at = pl.ds(pl.multiple_of((half * 2 + place_of) * rows, rows), rows)
             out[at, :] = part[half * rows : (half + 1) * rows, :]
+
+
+def routes(rows, width, args):
+    n_req = lax.axis_size("req")
+    n_experts = args[1].shape[0]
+    hidden, d_model = args[3].shape
+    hbm = pl.BlockSpec(memory_space=pltpu.HBM)
+    outs = [
+        like((n_experts, width), BF16),
+        like((2 * n_req, n_experts), F32),
+        like((2 * hidden, d_model), BF16),
+    ]
+    moves = 2 * hidden * d_model * 2
+    return pl.pallas_call(
+        lambda *refs: routes_kernel(rows, *refs),
+        out_shape=tuple(outs),
+        in_specs=[in_smem(), *in_vmem(2), hbm, hbm],
+        out_specs=tuple(in_vmem(3)),
+        scratch_shapes=[pltpu.SemaphoreType.DMA((2,))],
+        cost_estimate=pl.CostEstimate(flops=0, bytes_accessed=moves, transcendentals=0),
+        compiler_params=pltpu.CompilerParams(vmem_limit_bytes=VMEM_LIMIT),
+        name="routes",
+    )(*args[:3], *(pltpu.with_memory_space_constraint(arg, pltpu.HBM) for arg in args[3:]))
+
+
+def joined_rows(parts, rows=None):
+    rows = parts[0].shape[0] if rows is None else rows
+    out = like((len(parts) * rows, parts[0].shape[1]), parts[0].dtype)
+    return called(joined_kernel, parts, [out], flops=0)[0]
 
 
 def exchanged(parts, chips):
@@ -578,18 +625,13 @@
 
     blocks = attention(chips, queries, keys, values, lengths, out_weight, w_down, block)
     down, near_weight, blocks = blocks[5:], blocks[4], list(blocks[:4])
-    shares, serves = called(
-        routes_kernel,
-        (replica_map, expert_ids.T, gate_weights.T),
-        [like((n_experts, expert_ids.shape[0]), F32), like((2 * n_req, n_experts), F32)],
-        flops=0,
-        n_smem=1,
-    )
+    w_in = (w_gate[0].T, w_up[0].T)
+    tail, serves, w_near = routes(rows, 2 * block, (replica_map, expert_ids.T, gate_weights.T, *w_in))
     blocks[3] = moved(blocks[3], 0, 1, 1)
     blocks[1] = moved(blocks[1], 0, 0, 1)
     far_weight = moved(near_weight, 0, 1, 0)
     blocks[2] = moved(blocks[2], 0, 1, 0)
-    blocks[3], serves, shares = lax.optimization_barrier((blocks[3], serves, shares))
+    blocks[3], serves, tail = lax.optimization_barrier((blocks[3], serves, tail))
     wide = (rows, 2 * block)
     sums = called(
         lambda *refs: projection_kernel(chips, *refs),
@@ -598,16 +640,16 @@
         flops=4 * rows * out_weight.size,
         scratch=[pltpu.VMEM((rows, blocks[0].shape[1]), BF16)] * 2,
     )
-    w_in = [w_gate[0].T, w_up[0].T]
-    later, _ = lax.optimization_barrier((tuple(w_in), sums[1]))
-    w_in = [w_in[0], moved(later[0], 0, 1, 0), w_in[1], moved(later[1], 0, 1, 0)]
+    later, _ = lax.optimization_barrier((w_near, sums[1]))
+    w_far = moved(later, 0, 1, 0)
     down, _ = lax.optimization_barrier((tuple(down), sums[1]))
     sums = exchanged(sums, chips)
     down = exchanged(down, chips)
-    down_far = [moved(piece, 0, 1, 0) for piece in down]
+    down = joined_rows(down)
+    down_far = moved(down, 0, 1, 0)
     mixed, sent = called(
         lambda *refs: mixed_kernel(n_chips, *refs),
-        (*sums, gain, shares),
+        (*sums, gain, tail),
         [like(wide, F32), like((rows + n_experts, 2 * block), BF16)],
         flops=8 * rows * block,
     )
@@ -617,25 +659,21 @@
     order = [0, *order]
     terms = {}
     for groups in (tuple(order[:half]), tuple(order[half:])):
-        (joined,) = called(
-            joined_kernel,
-            [by_group[d_req] for d_req in groups],
-            [like((half * rows, 2 * block), BF16)],
-            flops=0,
-        )
+        n_rows = len(groups) * rows
+        joined = joined_rows([by_group[d_req] for d_req in groups], rows)
         parts = spread(joined, chips)
         (act,) = called(
             lambda *refs, groups=groups: expert_kernel(chips, groups, *refs),
-            (serves, gain, *w_in, *(by_group[d_req] for d_req in groups), *parts),
-            [like((half * rows, 2 * hidden), BF16)],
-            flops=8 * half * rows * d_model * hidden,
+            (serves, gain, w_near, w_far, *(by_group[d_req] for d_req in groups), *parts),
+            [like((n_rows, 2 * hidden), BF16)],
+            flops=8 * n_rows * d_model * hidden,
         )
-        tail = (mixed,) if 0 in groups else ()
+        own_mixed = (mixed,) if 0 in groups else ()
         results = called(
             lambda *refs, groups=groups: combine_kernel(n_chips, groups, *refs),
-            (*spread(act, chips), *down, *down_far, *tail),
+            (*spread(act, chips), down, down_far, *own_mixed),
             [like(wide, F32 if d_req == 0 else BF16) for d_req in groups],
-            flops=8 * half * rows * hidden * n_chips * block,
+            flops=8 * n_rows * hidden * n_chips * block,
         )
         for d_req, result in zip(groups, results, strict=True):
             terms[d_req] = moved(result, d_req, 0, 0) if d_req else result

time: 79.4 us -> 76.8 us (0.967)
  starting transfers between devices: 34.8 us -> 27.2 us
  waiting for transfers between devices: 34.4 us -> 39.6 us
  local copies, waits for them, and re-layouts: 1.49 us -> 0.02 us
  Pallas kernels: 8.41 us -> 9.68 us
    ppermute x35 -> x31, starting transfers between devices: 34.8 us -> 27.2 us  [moved(): return lax.ppermute(value, AXES, pairs)]
    ppermute x35 -> x31, waiting for transfers between devices: 34.4 us -> 39.6 us  [moved(): return lax.ppermute(value, AXES, pairs)]
    pallas_call x0 -> x1, Pallas kernels: none -> 2.03 us  [routes(): pl.pallas_call(lambda *refs: routes_kernel(rows, *refs), out_shape=tuple(...]
    unnamed x14 -> x10, local copies, waits for them, and re-layouts: 1.49 us -> 0.02 us
  transfers between devices with their start and end apart: 35 -> 31, of which waited for: 17 -> 18; matrix products, arithmetic and copies ran while one was open for 0% -> 0% of each run, Pallas kernels for 6% -> 8%
where the time goes in v2:
time: 76.8 us; the launch traced here: 76.6 us
  waiting for transfers between devices  39.6 us (52%)
  starting transfers between devices  27.2 us (35%)
  Pallas kernels  9.68 us (13%)
    ppermute x31, waiting for transfers between devices, moved(): return lax.ppermute(value, AXES, pairs)  39.6 us
    ppermute x31, starting transfers between devices, moved(): return lax.ppermute(value, AXES, pairs)  27.2 us
    pallas_call x11, Pallas kernels, called(): pl.pallas_call(kernel, out_shape=tuple(outs), in_specs=[in_smem()] * n_sm...  4.99 us
    pallas_call x1, Pallas kernels, attention(): pl.pallas_call(lambda *refs: attention_kernel(chips, *refs), out_shape=tu...  2.66 us
    pallas_call x1, Pallas kernels, routes(): pl.pallas_call(lambda *refs: routes_kernel(rows, *refs), out_shape=tuple(...  2.03 us
  transfers between devices with their start and end apart: 31, of which 18 were waited for; matrix products, arithmetic and copies ran while one was open for 0% of the time, Pallas kernels for 8%

profile of v2, /device:TPU:0, one launch (start us, length us, event | category | flops | bytes accessed | tf_op | source)
XLA Modules:
  0.0 76.6 jit_solution(5821796008087871170)
XLA Ops:
  0.0 2.7 %attention.1 = (bf16[32,256]{1,0:T(8,128)(2,1)S(1)}, bf16[32,256]{1,0:T(8,128)(2,1)S(1)}, bf16[32,256]{1,0:T(8,128)(2,1)S(1)}, bf16[32,256]{1,0:T(8,128)(2,1)S(1...) custom-call(s32[128]{0:T(128)} %refs_0_.2, ...), custom_call_target="tpu_custom_call" | custom-call | flops 201326592 | bytes 2097152 | tf_op jit(solution)/shard_map/attention/pallas_call | solution.py:342
  2.7 0.6 collective-permute-start.3
  3.2 2.6 %collective-permute-start = (bf16[32,256]{1,0:T(8,128)(2,1)S(1)}, bf16[32,256]{1,0:T(8,128)(2,1)S(1)}, u32[]{:S(2)}, u32[]{:S(2)}) collective-permute-start(bf16[32,256]{1,0:T(8,128)(2,1)S(1)} %get-tuple-element.37), channel_id=1, source_target_pairs={{0,3},{1,2},{2,1},{3,0},{4,7},{5,6},{6,5},{7,4},{8,11},{9,10},{10,... | collective-permute-start | bytes 49160 | tf_op jit(solution)/shard_map/ppermute | solution.py:202
  6.0 2.0 %routes.1 = (bf16[8,512]{1,0:T(8,128)(2,1)S(1)}, f32[8,8]{1,0:T(8,128)S(1)}, bf16[384,2048]{1,0:T(8,128)(2,1)S(1)}) custom-call(s32[16]{0:T(128)S(1)} %copy-done.4, s32[8,128]{1,0:T(8,128)S(1)} %bitcast.12, f32[8,128]{1,0:T(8,128)S(1)} %bitcast.13, bf16[192,2048]{1,0:T(8,128)(2,1)} %bitcast.14, bf16[192,2048]{1,0:T(8,128)(2,1)} %bitcast.15), custom_call_target="tpu_custom_call" | custom-call | bytes 1572864 | tf_op jit(solution)/shard_map/routes/pallas_call | solution.py:568
  8.0 1.6 %collective-permute-done.1.refs_1_ = bf16[32,256]{1,0:T(8,128)(2,1)S(1)} collective-permute-done((bf16[32,256]{1,0:T(8,128)(2,1)S(1)}, bf16[32,256]{1,0:T(8,128)(2,1)S(1)}, u32[]{:S(2)}, u32[]{:S(2)}) %collective-permute-start.1) | collective-permute-done | bytes 16416 | tf_op jit(solution)/shard_map/ppermute | solution.py:202
  9.6 0.5 shard_map.127
  10.2 0.9 %collective-permute-start.15 = (bf16[192,512]{1,0:T(8,128)(2,1)S(1)}, bf16[192,512]{1,0:T(8,128)(2,1)S(1)}, u32[]{:S(2)}, u32[]{:S(2)}) collective-permute-start(bf16[192,512]{1,0:T(8,128)(2,1)S(1)} %get-tuple-element.59), channel_id=1, source_target_pairs={{0,1},{1,0},{2,3},{3,2},{4,5},{5,4},{6,7},{7,6},{8,9},{9,8},{10,11... | collective-permute-start | bytes 589832 | tf_op jit(solution)/shard_map/ppermute | solution.py:202
  11.1 1.5 %collective-permute-start.16 = (bf16[192,512]{1,0:T(8,128)(2,1)S(1)}, bf16[192,512]{1,0:T(8,128)(2,1)S(1)}, u32[]{:S(2)}, u32[]{:S(2)}) collective-permute-start(bf16[192,512]{1,0:T(8,128)(2,1)S(1)} %get-tuple-element.60), channel_id=1, source_target_pairs={{0,4},{1,5},{2,6},{3,7},{4,0},{5,1},{6,2},{7,3},{8,12},{9,13},{10,... | collective-permute-start | bytes 589832 | tf_op jit(solution)/shard_map/ppermute | solution.py:202
  12.6 1.2 %collective-permute-start.17 = (bf16[192,512]{1,0:T(8,128)(2,1)S(1)}, bf16[192,512]{1,0:T(8,128)(2,1)S(1)}, u32[]{:S(2)}, u32[]{:S(2)}) collective-permute-start(bf16[192,512]{1,0:T(8,128)(2,1)S(1)} %get-tuple-element.61), channel_id=1, source_target_pairs={{0,5},{1,4},{2,7},{3,6},{4,1},{5,0},{6,3},{7,2},{8,13},{9,12},{10,... | collective-permute-start | bytes 589832 | tf_op jit(solution)/shard_map/ppermute | solution.py:202
  13.8 4.3 %collective-permute-done.15.refs_1_ = bf16[192,512]{1,0:T(8,128)(2,1)S(1)} collective-permute-done((bf16[192,512]{1,0:T(8,128)(2,1)S(1)}, bf16[192,512]{1,0:T(8,128)(2,1)S(1)}, u32[]{:S(2)}, u32[]{:S(2)}) %collective-permute-start.15) | collective-permute-done | bytes 196640 | tf_op jit(solution)/shard_map/ppermute | solution.py:202
  18.0 3.0 %collective-permute-done.16.refs_2_ = bf16[192,512]{1,0:T(8,128)(2,1)S(1)} collective-permute-done((bf16[192,512]{1,0:T(8,128)(2,1)S(1)}, bf16[192,512]{1,0:T(8,128)(2,1)S(1)}, u32[]{:S(2)}, u32[]{:S(2)}) %collective-permute-start.16) | collective-permute-done | bytes 196640 | tf_op jit(solution)/shard_map/ppermute | solution.py:202
  21.0 1.6 %collective-permute-done.17.refs_3_ = bf16[192,512]{1,0:T(8,128)(2,1)S(1)} collective-permute-done((bf16[192,512]{1,0:T(8,128)(2,1)S(1)}, bf16[192,512]{1,0:T(8,128)(2,1)S(1)}, u32[]{:S(2)}, u32[]{:S(2)}) %collective-permute-start.17) | collective-permute-done | bytes 196640 | tf_op jit(solution)/shard_map/ppermute | solution.py:202
  22.8 0.9 %collective-permute-start.5 = (bf16[64,512]{1,0:T(8,128)(2,1)S(1)}, bf16[64,512]{1,0:T(8,128)(2,1)S(1)}, u32[]{:S(2)}, u32[]{:S(2)}) collective-permute-start(bf16[64,512]{1,0:T(8,128)(2,1)S(1)} %get-tuple-element.47), channel_id=1, source_target_pairs={{0,1},{1,0},{2,3},{3,2},{4,5},{5,4},{6,7},{7,6},{8,9},{9,8},{10,11... | collective-permute-start | bytes 196616 | tf_op jit(solution)/shard_map/ppermute | solution.py:202
  23.7 1.5 %collective-permute-start.6 = (bf16[64,512]{1,0:T(8,128)(2,1)S(1)}, bf16[64,512]{1,0:T(8,128)(2,1)S(1)}, u32[]{:S(2)}, u32[]{:S(2)}) collective-permute-start(bf16[64,512]{1,0:T(8,128)(2,1)S(1)} %get-tuple-element.50), channel_id=1, source_target_pairs={{0,4},{1,5},{2,6},{3,7},{4,0},{5,1},{6,2},{7,3},{8,12},{9,13},{10,... | collective-permute-start | bytes 196616 | tf_op jit(solution)/shard_map/ppermute | solution.py:202
  25.2 1.2 %collective-permute-start.7 = (bf16[64,512]{1,0:T(8,128)(2,1)S(1)}, bf16[64,512]{1,0:T(8,128)(2,1)S(1)}, u32[]{:S(2)}, u32[]{:S(2)}) collective-permute-start(bf16[64,512]{1,0:T(8,128)(2,1)S(1)} %get-tuple-element.51), channel_id=1, source_target_pairs={{0,5},{1,4},{2,7},{3,6},{4,1},{5,0},{6,3},{7,2},{8,13},{9,12},{10,... | collective-permute-start | bytes 196616 | tf_op jit(solution)/shard_map/ppermute | solution.py:202
  26.4 0.9 %collective-permute-done.5.refs_1_ = bf16[64,512]{1,0:T(8,128)(2,1)S(1)} collective-permute-done((bf16[64,512]{1,0:T(8,128)(2,1)S(1)}, bf16[64,512]{1,0:T(8,128)(2,1)S(1)}, u32[]{:S(2)}, u32[]{:S(2)}) %collective-permute-start.5) | collective-permute-done | bytes 65568 | tf_op jit(solution)/shard_map/ppermute | solution.py:202
  27.3 0.6 collective-permute-done.6.refs_2_
  27.9 2.4 %collective-permute-done.7.refs_3_ = bf16[64,512]{1,0:T(8,128)(2,1)S(1)} collective-permute-done((bf16[64,512]{1,0:T(8,128)(2,1)S(1)}, bf16[64,512]{1,0:T(8,128)(2,1)S(1)}, u32[]{:S(2)}, u32[]{:S(2)}) %collective-permute-start.7) | collective-permute-done | bytes 65568 | tf_op jit(solution)/shard_map/ppermute | solution.py:202
  30.4 1.6 %collective-permute-start.8 = (bf16[72,512]{1,0:T(8,128)(2,1)S(1)}, bf16[72,512]{1,0:T(8,128)(2,1)S(1)}, u32[]{:S(2)}, u32[]{:S(2)}) collective-permute-start(bf16[72,512]{1,0:T(8,128)(2,1)S(1)} %get-tuple-element.53.refs_0_.refs_4_), channel_id=1, source_target_pairs={{0,8},{1,9},{2,10},{3,11},{4,12},{5,13},{6,14},{7,15},{8,0},{9,1},... | collective-permute-start | bytes 221192 | tf_op jit(solution)/shard_map/ppermute | solution.py:202
  32.0 2.6 %collective-permute-start.20 = (bf16[72,512]{1,0:T(8,128)(2,1)S(1)}, bf16[72,512]{1,0:T(8,128)(2,1)S(1)}, u32[]{:S(2)}, u32[]{:S(2)}) collective-permute-start(bf16[72,512]{1,0:T(8,128)(2,1)S(1)} %get-tuple-element.53.refs_0_.refs_4_), channel_id=1, source_target_pairs={{0,16},{1,17},{2,18},{3,19},{4,20},{5,21},{6,22},{7,23},{8,24},{9,... | collective-permute-start | bytes 221192 | tf_op jit(solution)/shard_map/ppermute | solution.py:202
  34.6 0.2 collective-permute-start.21
  34.9 0.6 collective-permute-done.8.refs_1_.refs_5_
  35.5 0.7 collective-permute-start.9
  36.2 2.7 %collective-permute-done.20.refs_0_.refs_4_ = bf16[72,512]{1,0:T(8,128)(2,1)S(1)} collective-permute-done((bf16[72,512]{1,0:T(8,128)(2,1)S(1)}, bf16[72,512]{1,0:T(8,128)(2,1)S(1)}, u32[]{:S(2)}, u32[]{:S(2)}) %collective-permute-start.20) | collective-permute-done | bytes 73760 | tf_op jit(solution)/shard_map/ppermute | solution.py:202
  38.9 0.5 collective-permute-start.10
  39.4 1.4 %collective-permute-done.21.refs_1_.refs_5_ = bf16[72,512]{1,0:T(8,128)(2,1)S(1)} collective-permute-done((bf16[72,512]{1,0:T(8,128)(2,1)S(1)}, bf16[72,512]{1,0:T(8,128)(2,1)S(1)}, u32[]{:S(2)}, u32[]{:S(2)}) %collective-permute-start.21) | collective-permute-done | bytes 73760 | tf_op jit(solution)/shard_map/ppermute | solution.py:202
  40.8 1.2 %collective-permute-start.11 = (bf16[128,512]{1,0:T(8,128)(2,1)S(1)}, bf16[128,512]{1,0:T(8,128)(2,1)S(1)}, u32[]{:S(2)}, u32[]{:S(2)}) collective-permute-start(bf16[128,512]{1,0:T(8,128)(2,1)S(1)} %shard_map.129.refs_6_), channel_id=1, source_target_pairs={{0,5},{1,4},{2,7},{3,6},{4,1},{5,0},{6,3},{7,2},{8,13},{9,12},{10,... | collective-permute-start | bytes 393224 | tf_op jit(solution)/shard_map/ppermute | solution.py:202
  42.0 0.9 %collective-permute-start.22 = (bf16[128,512]{1,0:T(8,128)(2,1)S(1)}, bf16[128,512]{1,0:T(8,128)(2,1)S(1)}, u32[]{:S(2)}, u32[]{:S(2)}) collective-permute-start(bf16[128,512]{1,0:T(8,128)(2,1)S(1)} %shard_map.133.refs_6_), channel_id=1, source_target_pairs={{0,1},{1,0},{2,3},{3,2},{4,5},{5,4},{6,7},{7,6},{8,9},{9,8},{10,11... | collective-permute-start | bytes 393224 | tf_op jit(solution)/shard_map/ppermute | solution.py:202
  42.8 5.4 %collective-permute-done.10.refs_8_ = bf16[128,512]{1,0:T(8,128)(2,1)S(1)} collective-permute-done((bf16[128,512]{1,0:T(8,128)(2,1)S(1)}, bf16[128,512]{1,0:T(8,128)(2,1)S(1)}, u32[]{:S(2)}, u32[]{:S(2)}) %collective-permute-start.10) | collective-permute-done | bytes 131104 | tf_op jit(solution)/shard_map/ppermute | solution.py:202
  48.3 1.9 %collective-permute-start.24 = (bf16[128,512]{1,0:T(8,128)(2,1)S(1)}, bf16[128,512]{1,0:T(8,128)(2,1)S(1)}, u32[]{:S(2)}, u32[]{:S(2)}) collective-permute-start(bf16[128,512]{1,0:T(8,128)(2,1)S(1)} %shard_map.133.refs_6_), channel_id=1, source_target_pairs={{0,5},{1,4},{2,7},{3,6},{4,1},{5,0},{6,3},{7,2},{8,13},{9,12},{10,... | collective-permute-start | bytes 393224 | tf_op jit(solution)/shard_map/ppermute | solution.py:202
  50.2 1.4 %shard_map.130.refs_0_ = bf16[128,384]{1,0:T(8,128)(2,1)S(1)} custom-call(f32[8,8]{1,0:T(8,128)S(1)} %get-tuple-element.40.refs_0_, f32[1,2048]{1,0:T(1,128)S(1)} %bitcast.10, bf16[384,2048]{1,0:T(8,128)(2,1)S(1)} %get-tuple-element.48.refs_2_, bf16[384,2048]{1,0:T(8,128)(2,1)S(1)} %collective-permute-done.4.refs_3_, ...), custom_call_target="tpu_custom_call" | custom-call | flops 402653184 | bytes 3924224 | tf_op jit(solution)/shard_map/pallas_call | solution.py:230
  51.6 1.6 %collective-permute-start.12 = (bf16[128,384]{1,0:T(8,128)(2,1)S(1)}, bf16[128,384]{1,0:T(8,128)(2,1)S(1)}, u32[]{:S(2)}, u32[]{:S(2)}) collective-permute-start(bf16[128,384]{1,0:T(8,128)(2,1)S(1)} %shard_map.130.refs_0_), channel_id=1, source_target_pairs={{0,1},{1,0},{2,3},{3,2},{4,5},{5,4},{6,7},{7,6},{8,9},{9,8},{10,11... | collective-permute-start | bytes 294920 | tf_op jit(solution)/shard_map/ppermute | solution.py:202
  53.3 4.2 %collective-permute-done.23.refs_8_ = bf16[128,512]{1,0:T(8,128)(2,1)S(1)} collective-permute-done((bf16[128,512]{1,0:T(8,128)(2,1)S(1)}, bf16[128,512]{1,0:T(8,128)(2,1)S(1)}, u32[]{:S(2)}, u32[]{:S(2)}) %collective-permute-start.23) | collective-permute-done | bytes 131104 | tf_op jit(solution)/shard_map/ppermute | solution.py:202
  57.5 0.6 collective-permute-start.14
  58.1 1.4 %shard_map.134.refs_0_ = bf16[128,384]{1,0:T(8,128)(2,1)S(1)} custom-call(f32[8,8]{1,0:T(8,128)S(1)} %get-tuple-element.40.refs_0_, f32[1,2048]{1,0:T(1,128)S(1)} %bitcast.11, bf16[384,2048]{1,0:T(8,128)(2,1)S(1)} %get-tuple-element.48.refs_2_, bf16[384,2048]{1,0:T(8,128)(2,1)S(1)} %collective-permute-done.4.refs_3_, ...), custom_call_target="tpu_custom_call" | custom-call | flops 402653184 | bytes 3924224 | tf_op jit(solution)/shard_map/pallas_call | solution.py:230
  59.5 0.3 collective-permute-start.25
  59.8 2.7 %collective-permute-start.26 = (bf16[128,384]{1,0:T(8,128)(2,1)S(1)}, bf16[128,384]{1,0:T(8,128)(2,1)S(1)}, u32[]{:S(2)}, u32[]{:S(2)}) collective-permute-start(bf16[128,384]{1,0:T(8,128)(2,1)S(1)} %shard_map.134.refs_0_), channel_id=1, source_target_pairs={{0,4},{1,5},{2,6},{3,7},{4,0},{5,1},{6,2},{7,3},{8,12},{9,13},{10,... | collective-permute-start | bytes 294920 | tf_op jit(solution)/shard_map/ppermute | solution.py:202
  62.4 0.6 collective-permute-start.27
  63.0 0.5 shard_map.132
  63.6 0.6 collective-permute-done.25.refs_1_
  64.1 0.9 %collective-permute-done.26.refs_2_ = bf16[128,384]{1,0:T(8,128)(2,1)S(1)} collective-permute-done((bf16[128,384]{1,0:T(8,128)(2,1)S(1)}, bf16[128,384]{1,0:T(8,128)(2,1)S(1)}, u32[]{:S(2)}, u32[]{:S(2)}) %collective-permute-start.26) | collective-permute-done | bytes 98336 | tf_op jit(solution)/shard_map/ppermute | solution.py:202
  65.0 2.9 %collective-permute-done.27.refs_3_ = bf16[128,384]{1,0:T(8,128)(2,1)S(1)} collective-permute-done((bf16[128,384]{1,0:T(8,128)(2,1)S(1)}, bf16[128,384]{1,0:T(8,128)(2,1)S(1)}, u32[]{:S(2)}, u32[]{:S(2)}) %collective-permute-start.27) | collective-permute-done | bytes 98336 | tf_op jit(solution)/shard_map/ppermute | solution.py:202
  67.9 0.4 shard_map.135
  68.5 1.0 %collective-permute-start.29 = (bf16[64,512]{1,0:T(8,128)(2,1)S(1)}, bf16[64,512]{1,0:T(8,128)(2,1)S(1)}, u32[]{:S(2)}, u32[]{:S(2)}) collective-permute-start(bf16[64,512]{1,0:T(8,128)(2,1)S(1)} %get-tuple-element.66), channel_id=1, source_target_pairs={{0,24},{1,25},{2,26},{3,27},{4,28},{5,29},{6,30},{7,31},{8,16},{9,... | collective-permute-start | bytes 196616 | tf_op jit(solution)/shard_map/ppermute | solution.py:202
  69.5 4.1 %collective-permute-done.28.refs_2_ = bf16[64,512]{1,0:T(8,128)(2,1)S(1)} collective-permute-done((bf16[64,512]{1,0:T(8,128)(2,1)S(1)}, bf16[64,512]{1,0:T(8,128)(2,1)S(1)}, u32[]{:S(2)}, u32[]{:S(2)}) %collective-permute-start.28) | collective-permute-done | bytes 65568 | tf_op jit(solution)/shard_map/ppermute | solution.py:202
  73.6 1.1 %collective-permute-done.29.refs_3_ = bf16[64,512]{1,0:T(8,128)(2,1)S(1)} collective-permute-done((bf16[64,512]{1,0:T(8,128)(2,1)S(1)}, bf16[64,512]{1,0:T(8,128)(2,1)S(1)}, u32[]{:S(2)}, u32[]{:S(2)}) %collective-permute-start.29) | collective-permute-done | bytes 65568 | tf_op jit(solution)/shard_map/ppermute | solution.py:202
  74.8 1.2 %collective-permute-done.30.other = bf16[64,256]{1,0:T(8,128)(2,1)S(1)} collective-permute-done((bf16[64,256]{1,0:T(8,128)(2,1)S(1)}, bf16[64,256]{1,0:T(8,128)(2,1)S(1)}, u32[]{:S(2)}, u32[]{:S(2)}) %collective-permute-start.30) | collective-permute-done | bytes 32800 | tf_op jit(solution)/shard_map/ppermute | solution.py:202
  76.0 0.6 shard_map.137
  (37 shorter events, 0.8 us)
Async XLA Ops:
  0.0 6.0 %copy-start.4 = (s32[16]{0:T(128)S(1)}, s32[16]{0:T(128)}, u32[]{:S(2)}) copy-start(s32[16]{0:T(128)} %refs_0_.3) | copy-start | bytes 196
  0.0 6.0 %copy-start.2 = (s32[128,8]{0,1:T(8,128)S(1)}, s32[128,8]{0,1:T(8,128)}, u32[]{:S(2)}) copy-start(s32[128,8]{0,1:T(8,128)} %param.20) | copy-start | bytes 12292
  0.0 6.0 %copy-start.3 = (f32[128,8]{0,1:T(8,128)S(1)}, f32[128,8]{0,1:T(8,128)}, u32[]{:S(2)}) copy-start(f32[128,8]{0,1:T(8,128)} %param.21) | copy-start | bytes 12292
  2.7 6.9 %copy-start = (bf16[128,2048]{1,0:T(8,128)(2,1)S(1)}, bf16[128,2048]{1,0:T(8,128)(2,1)}, u32[]{:S(2)}) copy-start(bf16[128,2048]{1,0:T(8,128)(2,1)} %refs_6_.1) | copy-start | bytes 1572868
  2.7 6.9 %collective-permute-start.3 = (bf16[256,2048]{1,0:T(8,128)(2,1)S(1)}, bf16[256,2048]{1,0:T(8,128)(2,1)S(1)}, u32[]{:S(2)}, u32[]{:S(2)}) collective-permute-start(bf16[256,2048]{1,0:T(8,128)(2,1)S(1)} %get-tuple-element.46.refs_4_), channel_id=1, source_target_pairs={{0,2},{1,3},{2,0},{3,1},{4,6},{5,7},{6,4},{7,5},{8,10},{9,11},{10,... | collective-permute-start | bytes 3145736 | tf_op jit(solution)/shard_map/ppermute | solution.py:202
  3.2 4.8 %collective-permute-start = (bf16[32,256]{1,0:T(8,128)(2,1)S(1)}, bf16[32,256]{1,0:T(8,128)(2,1)S(1)}, u32[]{:S(2)}, u32[]{:S(2)}) collective-permute-start(bf16[32,256]{1,0:T(8,128)(2,1)S(1)} %get-tuple-element.37), channel_id=1, source_target_pairs={{0,3},{1,2},{2,1},{3,0},{4,7},{5,6},{6,5},{7,4},{8,11},{9,10},{10,... | collective-permute-start | bytes 49160 | tf_op jit(solution)/shard_map/ppermute | solution.py:202
  5.8 3.7 %collective-permute-start.1 = (bf16[32,256]{1,0:T(8,128)(2,1)S(1)}, bf16[32,256]{1,0:T(8,128)(2,1)S(1)}, u32[]{:S(2)}, u32[]{:S(2)}) collective-permute-start(bf16[32,256]{1,0:T(8,128)(2,1)S(1)} %get-tuple-element.43), channel_id=1, source_target_pairs={{0,1},{1,0},{2,3},{3,2},{4,5},{5,4},{6,7},{7,6},{8,9},{9,8},{10,11... | collective-permute-start | bytes 49160 | tf_op jit(solution)/shard_map/ppermute | solution.py:202
  5.9 3.7 %collective-permute-start.2 = (bf16[32,256]{1,0:T(8,128)(2,1)S(1)}, bf16[32,256]{1,0:T(8,128)(2,1)S(1)}, u32[]{:S(2)}, u32[]{:S(2)}) collective-permute-start(bf16[32,256]{1,0:T(8,128)(2,1)S(1)} %get-tuple-element.44), channel_id=1, source_target_pairs={{0,2},{1,3},{2,0},{3,1},{4,6},{5,7},{6,4},{7,5},{8,10},{9,11},{10,... | collective-permute-start | bytes 49160 | tf_op jit(solution)/shard_map/ppermute | solution.py:202
  9.6 20.8 %copy-start.1 = (f32[2048]{0:T(1024)S(1)}, f32[2048]{0:T(1024)}, u32[]{:S(2)}) copy-start(f32[2048]{0:T(1024)} %param.19) | copy-start | bytes 24580
  10.1 40.1 %collective-permute-start.4 = (bf16[384,2048]{1,0:T(8,128)(2,1)S(1)}, bf16[384,2048]{1,0:T(8,128)(2,1)S(1)}, u32[]{:S(2)}, u32[]{:S(2)}) collective-permute-start(bf16[384,2048]{1,0:T(8,128)(2,1)S(1)} %get-tuple-element.48.refs_2_), channel_id=1, source_target_pairs={{0,2},{1,3},{2,0},{3,1},{4,6},{5,7},{6,4},{7,5},{8,10},{9,11},{10,... | collective-permute-start | bytes 4718600 | tf_op jit(solution)/shard_map/ppermute | solution.py:202
  10.2 7.8 %collective-permute-start.15 = (bf16[192,512]{1,0:T(8,128)(2,1)S(1)}, bf16[192,512]{1,0:T(8,128)(2,1)S(1)}, u32[]{:S(2)}, u32[]{:S(2)}) collective-permute-start(bf16[192,512]{1,0:T(8,128)(2,1)S(1)} %get-tuple-element.59), channel_id=1, source_target_pairs={{0,1},{1,0},{2,3},{3,2},{4,5},{5,4},{6,7},{7,6},{8,9},{9,8},{10,11... | collective-permute-start | bytes 589832 | tf_op jit(solution)/shard_map/ppermute | solution.py:202
  11.1 10.0 %collective-permute-start.16 = (bf16[192,512]{1,0:T(8,128)(2,1)S(1)}, bf16[192,512]{1,0:T(8,128)(2,1)S(1)}, u32[]{:S(2)}, u32[]{:S(2)}) collective-permute-start(bf16[192,512]{1,0:T(8,128)(2,1)S(1)} %get-tuple-element.60), channel_id=1, source_target_pairs={{0,4},{1,5},{2,6},{3,7},{4,0},{5,1},{6,2},{7,3},{8,12},{9,13},{10,... | collective-permute-start | bytes 589832 | tf_op jit(solution)/shard_map/ppermute | solution.py:202
  12.6 10.1 %collective-permute-start.17 = (bf16[192,512]{1,0:T(8,128)(2,1)S(1)}, bf16[192,512]{1,0:T(8,128)(2,1)S(1)}, u32[]{:S(2)}, u32[]{:S(2)}) collective-permute-start(bf16[192,512]{1,0:T(8,128)(2,1)S(1)} %get-tuple-element.61), channel_id=1, source_target_pairs={{0,5},{1,4},{2,7},{3,6},{4,1},{5,0},{6,3},{7,2},{8,13},{9,12},{10,... | collective-permute-start | bytes 589832 | tf_op jit(solution)/shard_map/ppermute | solution.py:202
  22.7 37.0 %collective-permute-start.18 = (bf16[768,512]{1,0:T(8,128)(2,1)S(1)}, bf16[768,512]{1,0:T(8,128)(2,1)S(1)}, u32[]{:S(2)}, u32[]{:S(2)}) collective-permute-start(bf16[768,512]{1,0:T(8,128)(2,1)S(1)} %shard_map.131.refs_4_), channel_id=1, source_target_pairs={{0,2},{1,3},{2,0},{3,1},{4,6},{5,7},{6,4},{7,5},{8,10},{9,11},{10,... | collective-permute-start | bytes 2359304 | tf_op jit(solution)/shard_map/ppermute | solution.py:202
  22.8 4.5 %collective-permute-start.5 = (bf16[64,512]{1,0:T(8,128)(2,1)S(1)}, bf16[64,512]{1,0:T(8,128)(2,1)S(1)}, u32[]{:S(2)}, u32[]{:S(2)}) collective-permute-start(bf16[64,512]{1,0:T(8,128)(2,1)S(1)} %get-tuple-element.47), channel_id=1, source_target_pairs={{0,1},{1,0},{2,3},{3,2},{4,5},{5,4},{6,7},{7,6},{8,9},{9,8},{10,11... | collective-permute-start | bytes 196616 | tf_op jit(solution)/shard_map/ppermute | solution.py:202
  23.7 4.3 %collective-permute-start.6 = (bf16[64,512]{1,0:T(8,128)(2,1)S(1)}, bf16[64,512]{1,0:T(8,128)(2,1)S(1)}, u32[]{:S(2)}, u32[]{:S(2)}) collective-permute-start(bf16[64,512]{1,0:T(8,128)(2,1)S(1)} %get-tuple-element.50), channel_id=1, source_target_pairs={{0,4},{1,5},{2,6},{3,7},{4,0},{5,1},{6,2},{7,3},{8,12},{9,13},{10,... | collective-permute-start | bytes 196616 | tf_op jit(solution)/shard_map/ppermute | solution.py:202
  25.2 5.2 %collective-permute-start.7 = (bf16[64,512]{1,0:T(8,128)(2,1)S(1)}, bf16[64,512]{1,0:T(8,128)(2,1)S(1)}, u32[]{:S(2)}, u32[]{:S(2)}) collective-permute-start(bf16[64,512]{1,0:T(8,128)(2,1)S(1)} %get-tuple-element.51), channel_id=1, source_target_pairs={{0,5},{1,4},{2,7},{3,6},{4,1},{5,0},{6,3},{7,2},{8,13},{9,12},{10,... | collective-permute-start | bytes 196616 | tf_op jit(solution)/shard_map/ppermute | solution.py:202
  30.4 5.1 %collective-permute-start.8 = (bf16[72,512]{1,0:T(8,128)(2,1)S(1)}, bf16[72,512]{1,0:T(8,128)(2,1)S(1)}, u32[]{:S(2)}, u32[]{:S(2)}) collective-permute-start(bf16[72,512]{1,0:T(8,128)(2,1)S(1)} %get-tuple-element.53.refs_0_.refs_4_), channel_id=1, source_target_pairs={{0,8},{1,9},{2,10},{3,11},{4,12},{5,13},{6,14},{7,15},{8,0},{9,1},... | collective-permute-start | bytes 221192 | tf_op jit(solution)/shard_map/ppermute | solution.py:202
  32.0 6.8 %collective-permute-start.20 = (bf16[72,512]{1,0:T(8,128)(2,1)S(1)}, bf16[72,512]{1,0:T(8,128)(2,1)S(1)}, u32[]{:S(2)}, u32[]{:S(2)}) collective-permute-start(bf16[72,512]{1,0:T(8,128)(2,1)S(1)} %get-tuple-element.53.refs_0_.refs_4_), channel_id=1, source_target_pairs={{0,16},{1,17},{2,18},{3,19},{4,20},{5,21},{6,22},{7,23},{8,24},{9,... | collective-permute-start | bytes 221192 | tf_op jit(solution)/shard_map/ppermute | solution.py:202
  34.6 6.2 %collective-permute-start.21 = (bf16[72,512]{1,0:T(8,128)(2,1)S(1)}, bf16[72,512]{1,0:T(8,128)(2,1)S(1)}, u32[]{:S(2)}, u32[]{:S(2)}) collective-permute-start(bf16[72,512]{1,0:T(8,128)(2,1)S(1)} %get-tuple-element.53.refs_0_.refs_4_), channel_id=1, source_target_pairs={{0,24},{1,25},{2,26},{3,27},{4,28},{5,29},{6,30},{7,31},{8,16},{9,... | collective-permute-start | bytes 221192 | tf_op jit(solution)/shard_map/ppermute | solution.py:202
  35.5 6.5 %collective-permute-start.9 = (bf16[128,512]{1,0:T(8,128)(2,1)S(1)}, bf16[128,512]{1,0:T(8,128)(2,1)S(1)}, u32[]{:S(2)}, u32[]{:S(2)}) collective-permute-start(bf16[128,512]{1,0:T(8,128)(2,1)S(1)} %shard_map.129.refs_6_), channel_id=1, source_target_pairs={{0,1},{1,0},{2,3},{3,2},{4,5},{5,4},{6,7},{7,6},{8,9},{9,8},{10,11... | collective-permute-start | bytes 393224 | tf_op jit(solution)/shard_map/ppermute | solution.py:202
  38.9 9.4 %collective-permute-start.10 = (bf16[128,512]{1,0:T(8,128)(2,1)S(1)}, bf16[128,512]{1,0:T(8,128)(2,1)S(1)}, u32[]{:S(2)}, u32[]{:S(2)}) collective-permute-start(bf16[128,512]{1,0:T(8,128)(2,1)S(1)} %shard_map.129.refs_6_), channel_id=1, source_target_pairs={{0,4},{1,5},{2,6},{3,7},{4,0},{5,1},{6,2},{7,3},{8,12},{9,13},{10,... | collective-permute-start | bytes 393224 | tf_op jit(solution)/shard_map/ppermute | solution.py:202
  40.8 7.6 %collective-permute-start.11 = (bf16[128,512]{1,0:T(8,128)(2,1)S(1)}, bf16[128,512]{1,0:T(8,128)(2,1)S(1)}, u32[]{:S(2)}, u32[]{:S(2)}) collective-permute-start(bf16[128,512]{1,0:T(8,128)(2,1)S(1)} %shard_map.129.refs_6_), channel_id=1, source_target_pairs={{0,5},{1,4},{2,7},{3,6},{4,1},{5,0},{6,3},{7,2},{8,13},{9,12},{10,... | collective-permute-start | bytes 393224 | tf_op jit(solution)/shard_map/ppermute | solution.py:202
  42.0 11.2 %collective-permute-start.22 = (bf16[128,512]{1,0:T(8,128)(2,1)S(1)}, bf16[128,512]{1,0:T(8,128)(2,1)S(1)}, u32[]{:S(2)}, u32[]{:S(2)}) collective-permute-start(bf16[128,512]{1,0:T(8,128)(2,1)S(1)} %shard_map.133.refs_6_), channel_id=1, source_target_pairs={{0,1},{1,0},{2,3},{3,2},{4,5},{5,4},{6,7},{7,6},{8,9},{9,8},{10,11... | collective-permute-start | bytes 393224 | tf_op jit(solution)/shard_map/ppermute | solution.py:202
  48.3 9.2 %collective-permute-start.23 = (bf16[128,512]{1,0:T(8,128)(2,1)S(1)}, bf16[128,512]{1,0:T(8,128)(2,1)S(1)}, u32[]{:S(2)}, u32[]{:S(2)}) collective-permute-start(bf16[128,512]{1,0:T(8,128)(2,1)S(1)} %shard_map.133.refs_6_), channel_id=1, source_target_pairs={{0,4},{1,5},{2,6},{3,7},{4,0},{5,1},{6,2},{7,3},{8,12},{9,13},{10,... | collective-permute-start | bytes 393224 | tf_op jit(solution)/shard_map/ppermute | solution.py:202
  48.3 9.7 %collective-permute-start.24 = (bf16[128,512]{1,0:T(8,128)(2,1)S(1)}, bf16[128,512]{1,0:T(8,128)(2,1)S(1)}, u32[]{:S(2)}, u32[]{:S(2)}) collective-permute-start(bf16[128,512]{1,0:T(8,128)(2,1)S(1)} %shard_map.133.refs_6_), channel_id=1, source_target_pairs={{0,5},{1,4},{2,7},{3,6},{4,1},{5,0},{6,3},{7,2},{8,13},{9,12},{10,... | collective-permute-start | bytes 393224 | tf_op jit(solution)/shard_map/ppermute | solution.py:202
  51.6 10.8 %collective-permute-start.12 = (bf16[128,384]{1,0:T(8,128)(2,1)S(1)}, bf16[128,384]{1,0:T(8,128)(2,1)S(1)}, u32[]{:S(2)}, u32[]{:S(2)}) collective-permute-start(bf16[128,384]{1,0:T(8,128)(2,1)S(1)} %shard_map.130.refs_0_), channel_id=1, source_target_pairs={{0,1},{1,0},{2,3},{3,2},{4,5},{5,4},{6,7},{7,6},{8,9},{9,8},{10,11... | collective-permute-start | bytes 294920 | tf_op jit(solution)/shard_map/ppermute | solution.py:202
  53.2 9.8 %collective-permute-start.13 = (bf16[128,384]{1,0:T(8,128)(2,1)S(1)}, bf16[128,384]{1,0:T(8,128)(2,1)S(1)}, u32[]{:S(2)}, u32[]{:S(2)}) collective-permute-start(bf16[128,384]{1,0:T(8,128)(2,1)S(1)} %shard_map.130.refs_0_), channel_id=1, source_target_pairs={{0,4},{1,5},{2,6},{3,7},{4,0},{5,1},{6,2},{7,3},{8,12},{9,13},{10,... | collective-permute-start | bytes 294920 | tf_op jit(solution)/shard_map/ppermute | solution.py:202
  57.5 5.6 %collective-permute-start.14 = (bf16[128,384]{1,0:T(8,128)(2,1)S(1)}, bf16[128,384]{1,0:T(8,128)(2,1)S(1)}, u32[]{:S(2)}, u32[]{:S(2)}) collective-permute-start(bf16[128,384]{1,0:T(8,128)(2,1)S(1)} %shard_map.130.refs_0_), channel_id=1, source_target_pairs={{0,5},{1,4},{2,7},{3,6},{4,1},{5,0},{6,3},{7,2},{8,13},{9,12},{10,... | collective-permute-start | bytes 294920 | tf_op jit(solution)/shard_map/ppermute | solution.py:202
  59.5 4.7 %collective-permute-start.25 = (bf16[128,384]{1,0:T(8,128)(2,1)S(1)}, bf16[128,384]{1,0:T(8,128)(2,1)S(1)}, u32[]{:S(2)}, u32[]{:S(2)}) collective-permute-start(bf16[128,384]{1,0:T(8,128)(2,1)S(1)} %shard_map.134.refs_0_), channel_id=1, source_target_pairs={{0,1},{1,0},{2,3},{3,2},{4,5},{5,4},{6,7},{7,6},{8,9},{9,8},{10,11... | collective-permute-start | bytes 294920 | tf_op jit(solution)/shard_map/ppermute | solution.py:202
  59.8 5.3 %collective-permute-start.26 = (bf16[128,384]{1,0:T(8,128)(2,1)S(1)}, bf16[128,384]{1,0:T(8,128)(2,1)S(1)}, u32[]{:S(2)}, u32[]{:S(2)}) collective-permute-start(bf16[128,384]{1,0:T(8,128)(2,1)S(1)} %shard_map.134.refs_0_), channel_id=1, source_target_pairs={{0,4},{1,5},{2,6},{3,7},{4,0},{5,1},{6,2},{7,3},{8,12},{9,13},{10,... | collective-permute-start | bytes 294920 | tf_op jit(solution)/shard_map/ppermute | solution.py:202
  62.4 5.5 %collective-permute-start.27 = (bf16[128,384]{1,0:T(8,128)(2,1)S(1)}, bf16[128,384]{1,0:T(8,128)(2,1)S(1)}, u32[]{:S(2)}, u32[]{:S(2)}) collective-permute-start(bf16[128,384]{1,0:T(8,128)(2,1)S(1)} %shard_map.134.refs_0_), channel_id=1, source_target_pairs={{0,5},{1,4},{2,7},{3,6},{4,1},{5,0},{6,3},{7,2},{8,13},{9,12},{10,... | collective-permute-start | bytes 294920 | tf_op jit(solution)/shard_map/ppermute | solution.py:202
  63.5 6.0 %collective-permute-start.19 = (bf16[64,512]{1,0:T(8,128)(2,1)S(1)}, bf16[64,512]{1,0:T(8,128)(2,1)S(1)}, u32[]{:S(2)}, u32[]{:S(2)}) collective-permute-start(bf16[64,512]{1,0:T(8,128)(2,1)S(1)} %get-tuple-element.64), channel_id=1, source_target_pairs={{0,8},{1,9},{2,10},{3,11},{4,12},{5,13},{6,14},{7,15},{8,0},{9,1},... | collective-permute-start | bytes 196616 | tf_op jit(solution)/shard_map/ppermute | solution.py:202
  68.4 5.2 %collective-permute-start.28 = (bf16[64,512]{1,0:T(8,128)(2,1)S(1)}, bf16[64,512]{1,0:T(8,128)(2,1)S(1)}, u32[]{:S(2)}, u32[]{:S(2)}) collective-permute-start(bf16[64,512]{1,0:T(8,128)(2,1)S(1)} %get-tuple-element.65), channel_id=1, source_target_pairs={{0,16},{1,17},{2,18},{3,19},{4,20},{5,21},{6,22},{7,23},{8,24},{9,... | collective-permute-start | bytes 196616 | tf_op jit(solution)/shard_map/ppermute | solution.py:202
  68.5 6.2 %collective-permute-start.29 = (bf16[64,512]{1,0:T(8,128)(2,1)S(1)}, bf16[64,512]{1,0:T(8,128)(2,1)S(1)}, u32[]{:S(2)}, u32[]{:S(2)}) collective-permute-start(bf16[64,512]{1,0:T(8,128)(2,1)S(1)} %get-tuple-element.66), channel_id=1, source_target_pairs={{0,24},{1,25},{2,26},{3,27},{4,28},{5,29},{6,30},{7,31},{8,16},{9,... | collective-permute-start | bytes 196616 | tf_op jit(solution)/shard_map/ppermute | solution.py:202
  74.7 1.3 %collective-permute-start.30 = (bf16[64,256]{1,0:T(8,128)(2,1)S(1)}, bf16[64,256]{1,0:T(8,128)(2,1)S(1)}, u32[]{:S(2)}, u32[]{:S(2)}) collective-permute-start(bf16[64,256]{1,0:T(8,128)(2,1)S(1)} %get-tuple-element.68), channel_id=1, source_target_pairs={{0,2},{1,3},{2,0},{3,1},{4,6},{5,7},{6,4},{7,5},{8,10},{9,11},{10,... | collective-permute-start | bytes 98312 | tf_op jit(solution)/shard_map/ppermute | solution.py:202
